TPU v7x, 128 devices: a whole 4x4x4 slice. The times are simulated.
128 devices in a mesh: grp: 4 (over z), dom: 32 (over y, x, core).
Axes of the slice: x: 4, y: 4, z: 4, core: 2. Of those that a mesh axis runs over, the one named last changes fastest.
Arguments:
- fluid_start: float32 [4, 1024, 96, 128], P('grp', 'dom'), may hold values from -6 to 6
- fluid_rate: float32 [4, 1024, 96, 128], P('grp', 'dom'), may hold values from 0.15 to 0.45
- fluid_coupling: float32 [4, 1024, 128], P('grp', 'dom'), may hold values from 0.1 to 0.5
- solid_start: float32 [4, 512, 24, 128], P('grp', 'dom'), may hold values from -6 to 6
- solid_rate: float32 [4, 512, 24, 128], P('grp', 'dom'), may hold values from 0.2 to 0.6
- solid_coupling: float32 [4, 512, 128], P('grp', 'dom'), may hold values from 0.1 to 0.5
- solid_block: int32 [12288], P(('grp', 'dom')), may hold values from 0 to 511, as said below
- to_solid: bfloat16 [12288, 128, 128], P(('grp', 'dom')), as said below
- to_fluid: bfloat16 [12288, 128, 128], P(('grp', 'dom')), as said below
Outputs:
- fluid_temp: float32 [4, 1024, 96, 128], P('grp', 'dom')
- solid_temp: float32 [4, 512, 24, 128], P('grp', 'dom')
Inputs may be any that keep to these rules, and one draw needn't show every extreme that they name: For segment s of fluid block x of its zone (x = (s // 3) mod 1024), solid_block[s] lies within x // 2 - 2 to x // 2 + 2, taken modulo 512. `to_solid`: entry [s, i, j] is zero unless i and j differ by at most one; all entries are nonnegative. `to_fluid`: entry [s, i, j] is zero unless i and j differ by at most one; all entries are nonnegative.
All inputs are finite; a program needn't handle non-finite values.
Results may differ from a plain program's by a relative error of at most 0.0003.
Values may be sent and summed in bfloat16 or wider, within the bound.
A program may use at most 128 MiB of HBM per device.

v0:
```python
import jax
import jax.numpy as jnp
from jax import lax
from jax.experimental import pallas as pl
from jax.experimental.pallas import tpu as pltpu
from jax.sharding import PartitionSpec as P

MESH = pl.DeviceIdType.MESH
F32 = jnp.float32
BF16 = jnp.bfloat16
FX, FY, FZ = 32, 96, 128
SX, SY = 16, 24
SEG = 96
GROUP = 16


def lane_iota(shape):
    return lax.broadcasted_iota(jnp.int32, shape, 1)


def zsum(v):
    lane = lane_iota(v.shape)
    return jnp.where(lane == 0, 0.0, pltpu.roll(v, 1, 1)) + jnp.where(
        lane == FZ - 1, 0.0, pltpu.roll(v, FZ - 1, 1)
    )


def ysum(v):
    zero = jnp.zeros((1, FZ), F32)
    return jnp.concatenate([zero, v[:-1]], axis=0) + jnp.concatenate([v[1:], zero], axis=0)


def rows_loop(lo, hi, unroll, body):
    count = hi - lo
    groups = count // unroll if count > unroll else 0
    if groups:

        def step(i, carry):
            for j in range(unroll):
                body(lo + i * unroll + j)
            return carry

        lax.fori_loop(0, groups, step, 0)
    for x in range(lo + groups * unroll, hi):
        body(x)


def at_row(x, pitch):
    return x * pitch if isinstance(x, int) else pl.multiple_of(x * pitch, 8)


def to_f32(v):
    return v.astype(F32)


def rounded(v):
    return v.astype(BF16).astype(F32)


def kernel(
    n_grp, n_dom,
    fs, fr, fc, ss, sr, sc, sb, ts, tf,
    fo, so,
    p, q, a, b, bt, sp, sq, sa, sbb, sbt,
    mt, yy, xf0, xf1, xf2, xr, xa, xb, xs0, xs1, xsr, xsa, xsb,
    dx, vv, ww, pad, tpad, fin, sin, sins, fxx, fsx, xoff,
    fcv, scv, sbv,
    ifs, is_, wb, bhl, bhr, shl, shr, mhl, mhr,
    rfl, rfr, fcl, fcr, sbl, sbr, rso, rsr, rsl, sco, scr, scl, scbr, scbl,
    wr, wl, bhrr, bhlr, shrr, shlr, mhrr, mhlr, sinr,
    load_sem, send_sem, recv_sem,
):
    g = lax.axis_index("grp")
    d = lax.axis_index("dom")
    gm, gp = lax.rem(g + n_grp - 1, n_grp), lax.rem(g + 1, n_grp)
    dm, dp = lax.rem(d + n_dom - 1, n_dom), lax.rem(d + 1, n_dom)
    ml = jnp.where(d > 0, 1.0, 0.0).astype(F32)
    mr = jnp.where(d < n_dom - 1, 1.0, 0.0).astype(F32)

    barrier = pltpu.get_barrier_semaphore()
    peers = ((g, dm), (g, dp), (gm, d), (gp, d), (gm, dm), (gm, dp), (gp, dm), (gp, dp))
    for peer in peers:
        pl.semaphore_signal(barrier, inc=1, device_id=peer, device_id_type=MESH)

    loads = {}

    def load(name, src, dst, index):
        loads[name] = pltpu.make_async_copy(src, dst, load_sem.at[index])
        loads[name].start()

    load("ss", ss, sp.at[pl.ds(8 * SY, SX * SY)], 0)
    load("sr", sr, sa.at[pl.ds(8 * SY, SX * SY)], 1)
    load("fs", fs, p.at[pl.ds(4 * FY, FX * FY)], 2)
    load("fr", fr, a.at[pl.ds(4 * FY, FX * FY)], 3)
    load("sc", sc, scv, 4)
    load("fc", fc, fcv, 5)
    load("sb", sb, sbv, 6)
    chunk = GROUP * FZ
    for t, src in ((0, ts), (1, tf)):
        for c in range(SEG // GROUP):
            load(
                ("m", t, c), src.at[pl.ds(c * chunk, chunk)],
                mt.at[pl.ds((t * SEG * FZ) + c * chunk, chunk)], 7 + t * 6 + c,
            )

    sends = []

    def send(src, dst, index, peer):
        copy = pltpu.make_async_remote_copy(
            src_ref=src, dst_ref=dst, send_sem=send_sem.at[index], recv_sem=recv_sem.at[index],
            device_id=peer, device_id_type=MESH,
        )
        copy.start()
        sends.append(copy)
        return copy

    loads["ss"].wait()
    loads["sr"].wait()
    for f, ref in ((0, sp), (1, sa)):
        for i in range(SX // 2):
            lo = (8 + 2 * i) * SY + 16
            is_[f, pl.ds(16 * i, 16), :] = jnp.concatenate(
                [ref[pl.ds(lo, 8), :], ref[pl.ds(lo + SY, 8), :]], axis=0
            ).astype(BF16)
        shl[f] = ref[pl.ds(8 * SY, 8 * SY), :].astype(BF16)
        shr[f] = ref[pl.ds(16 * SY, 8 * SY), :].astype(BF16)
    loads["fs"].wait()
    loads["fr"].wait()
    for f, ref in ((0, p), (1, a)):
        for i in range(FX // 2):
            lo = (4 + 2 * i) * FY
            pair = jnp.concatenate([ref[pl.ds(lo, 8), :], ref[pl.ds(lo + FY, 8), :]], axis=0)
            ifs[f, pl.ds(16 * i, 16), :] = pair.astype(BF16)
            own = xf0 if f == 0 else xr
            own[pl.ds((FX + 2 * i) * 8, 16), :] = pair
    loads["sc"].wait()
    loads["fc"].wait()
    loads["sb"].wait()
    pl.semaphore_wait(barrier, 8)

    recv = {}
    recv["rso"] = send(is_, rso, 6, (gm, d))
    recv["rsr"] = send(is_, rsr, 7, (gm, dm))
    recv["rsl"] = send(is_, rsl, 8, (gm, dp))
    recv["rfr"] = send(ifs.at[:, pl.ds(0, 192)], rfr, 0, (g, dm))
    recv["rfl"] = send(ifs.at[:, pl.ds(64, 192)], rfl, 1, (g, dp))
    recv["fcr"] = send(fcv, fcr, 2, (g, dm))
    recv["fcl"] = send(fcv, fcl, 3, (g, dp))
    recv["sbr"] = send(sbv, sbr, 4, (g, dm))
    recv["sbl"] = send(sbv, sbl, 5, (g, dp))
    recv["sco"] = send(scv, sco, 9, (gm, d))
    recv["scr"] = send(scv, scr, 10, (gm, dm))
    recv["scl"] = send(scv, scl, 11, (gm, dp))
    recv["scbr"] = send(scv, scbr, 12, (g, dm))
    recv["scbl"] = send(scv, scbl, 13, (g, dp))

    prow = lax.broadcasted_iota(jnp.int32, (8, FZ), 0)
    pcol = lane_iota((8, FZ))
    probe = jnp.where(lax.rem(pcol, 3) == prow, 1.0, 0.0).astype(BF16)
    for t in range(2):
        for c in range(SEG // GROUP):
            loads[("m", t, c)].wait()
            for s in range(GROUP):
                at = t * SEG + c * GROUP + s
                yy[pl.ds(at * 8, 8), :] = jnp.dot(
                    probe, mt[pl.ds(at * FZ, FZ), :], preferred_element_type=F32
                )
        y3 = [yy[pl.ds(t * SEG * 8 + c, SEG, stride=8), :] for c in range(3)]
        phase = lax.rem(lane_iota((SEG, FZ)), 3)
        for k, shift in enumerate((0, 2, 1)):
            picked = y3[(0 + shift) % 3]
            picked = jnp.where(phase == 1, y3[(1 + shift) % 3], picked)
            picked = jnp.where(phase == 2, y3[(2 + shift) % 3], picked)
            if k == 1:
                picked = jnp.where(lane_iota((SEG, FZ)) == 0, 0.0, picked)
            if k == 2:
                picked = jnp.where(lane_iota((SEG, FZ)) == FZ - 1, 0.0, picked)
            dx[3 * t + k, pl.ds(SEG, SEG), :] = picked
            wb[3 * t + k] = picked.astype(BF16)
    recv["wr"] = send(wb.at[:, pl.ds(0, 80)], wr, 14, (g, dm))
    recv["wl"] = send(wb.at[:, pl.ds(16, 80)], wl, 15, (g, dp))

    for i in range(4):
        bhl[pl.ds(i * FY, FY), :] = p[pl.ds((4 + i) * FY, FY), :].astype(BF16)
        bhr[pl.ds(i * FY, FY), :] = p[pl.ds((32 + i) * FY, FY), :].astype(BF16)
    for i in range(3):
        bhl[pl.ds((4 + i) * FY, FY), :] = a[pl.ds((4 + i) * FY, FY), :].astype(BF16)
        bhr[pl.ds((4 + i) * FY, FY), :] = a[pl.ds((33 + i) * FY, FY), :].astype(BF16)
    recv["bhrr"] = send(bhl, bhrr, 16, (g, dm))
    recv["bhlr"] = send(bhr, bhlr, 17, (g, dp))
    recv["shrr"] = send(shl, shrr, 18, (g, dm))
    recv["shlr"] = send(shr, shlr, 19, (g, dp))

    def coef(start_ref, rate_ref, a_ref, b_ref, lo, size):
        r = rate_ref[pl.ds(lo, size), :]
        inv = 1.0 / (1.0 + 6.0 * r)
        b_ref[pl.ds(lo, size), :] = start_ref[pl.ds(lo, size), :] * inv
        a_ref[pl.ds(lo, size), :] = r * inv

    def film_coef(r0, s0, film):
        inv0 = 1.0 / (1.0 + 6.0 * r0 + film)
        return r0 * inv0, s0 * inv0, film * inv0

    own_rows = pl.ds(4 * FY, FX, stride=FY)
    a0, b0, _ = film_coef(a[own_rows, :], p[own_rows, :], fcv[...])
    rows_loop(4, 36, 4, lambda x: coef(p, a, a, b, at_row(x, FY), FY))
    a[own_rows, :] = a0
    b[own_rows, :] = b0

    def fluid_row(src, dst, variant, x):
        base = at_row(x, FY)
        cur = src[pl.ds(base, FY), :]
        summed = src[pl.ds(base - FY, FY), :] + src[pl.ds(base + FY, FY), :]
        summed = summed + ysum(cur) + zsum(cur)
        if variant is None:
            fixed = b[pl.ds(base, FY), :]
        else:
            low = bt[pl.ds(variant * 320 + at_row(x, 8), 8), :]
            fixed = jnp.concatenate([low, b[pl.ds(base + 8, FY - 8), :]], axis=0)
        dst[pl.ds(base, FY), :] = fixed + a[pl.ds(base, FY), :] * summed

    def interior(variants):
        for m in range(4):
            src, dst = (p, q) if m % 2 == 0 else (q, p)
            rows_loop(
                5 + m, 35 - m, 8, lambda x: fluid_row(src, dst, variants[m], x)
            )

    def edges(variants):
        for m in range(4):
            src, dst = (p, q) if m % 2 == 0 else (q, p)
            for x0 in (1 + m, 35 - m):
                for x in range(x0, x0 + 4):
                    fluid_row(src, dst, variants[m], x)

    interior((None,) * 4)

    recv["rfl"].wait_recv()
    recv["rfr"].wait_recv()
    recv["fcl"].wait_recv()
    recv["fcr"].wait_recv()
    for f, ref in ((0, xf0), (1, xr)):
        ref[pl.ds(64, 192), :] = to_f32(rfl[f])
        ref[pl.ds(512, 192), :] = to_f32(rfr[f])
    fxx[pl.ds(0, FX), :] = fcl[...]
    fxx[pl.ds(FX, FX), :] = fcv[...]
    fxx[pl.ds(2 * FX, FX), :] = fcr[...]
    rows_loop(1, 11, 2, lambda x: coef(xf0, xr, xa, xb, at_row(x, 64), 64))
    xc = []
    xb0 = []
    for par in range(2):
        rows = pl.ds(par * 8, 48, stride=16)
        film = fxx[pl.ds(par, 48, stride=2), :]
        a0, b0, c0 = film_coef(xr[rows, :], xf0[rows, :], film)
        xa[rows, :] = a0
        fin[par] = b0
        fin[2 + par] = c0
        xc.append(2 + par)
        xb0.append(par)

    for name in ("rso", "rsr", "rsl", "sco", "scr", "scl"):
        recv[name].wait_recv()
    for f, ref in ((0, xs0), (1, xsr)):
        ref[pl.ds(0, 128), :] = to_f32(rsl[f])
        ref[pl.ds(128, 128), :] = to_f32(rso[f])
        ref[pl.ds(256, 128), :] = to_f32(rsr[f])
    rows_loop(0, 6, 2, lambda x: coef(xs0, xsr, xsa, xsb, at_row(x, 64), 64))
    srows = pl.ds(7, 48, stride=8)
    film = jnp.concatenate([scl[...], sco[...], scr[...]], axis=0)
    a0, b0, c0 = film_coef(xsr[srows, :], xs0[srows, :], film)
    xsa[srows, :] = a0
    sin[0] = b0
    sin[1] = c0

    for name in ("sbl", "sbr", "wl", "wr"):
        recv[name].wait_recv()
    for k in range(6):
        dx[k, pl.ds(16, 80), :] = to_f32(wl[k])
        dx[k, pl.ds(192, 80), :] = to_f32(wr[k])
    for n, ref in enumerate((sbl, sbv, sbr)):
        spread = jnp.broadcast_to(ref[...].astype(F32), (FZ, FZ)).T
        xoff[pl.ds(n * SEG, SEG), :] = spread[:SEG].astype(jnp.int32)
    first = SX * (d + n_dom - 1) - 2
    zone = SX * n_dom
    half = lax.broadcasted_iota(jnp.int32, (48, FZ), 0) + first
    for par in range(2):
        offs = [
            lax.rem(xoff[pl.ds(3 * par + j, 48, stride=6), :] - half + 3 * zone, zone)
            for j in range(3)
        ]
        for t in range(2):
            for k in range(3):
                diag = [dx[3 * t + k, pl.ds(3 * par + j, 48, stride=6), :] for j in range(3)]
                for o in range(5):
                    total = jnp.where(offs[0] == o, diag[0], 0.0)
                    total = total + jnp.where(offs[1] == o, diag[1], 0.0)
                    total = total + jnp.where(offs[2] == o, diag[2], 0.0)
                    at = (o * 3 + k) * 2 + par
                    if t == 0:
                        ww[at] = total
                    else:
                        vv[at] = total * fin[xc[par]]

    def shifts(v):
        return (v, pltpu.roll(v, 1, 1), pltpu.roll(v, FZ - 1, 1))

    def project_fluid(solid_ref, k):
        for n, v in enumerate(shifts(rounded(solid_ref[srows, :]))):
            pad[n, pl.ds(8, 48), :] = v
        for par in range(2):
            total = jnp.zeros((48, FZ), F32)
            for o in range(5):
                for n in range(3):
                    total = total + vv[(o * 3 + n) * 2 + par] * pad[n, pl.ds(6 + o, 48), :]
            fin[4 + 2 * k + par] = total

    def project_solid(fluid_ref, k):
        faces = [shifts(rounded(fluid_ref[pl.ds(par * 8, 48, stride=16), :])) for par in range(2)]
        for o in range(5):
            total = jnp.zeros((48, FZ), F32)
            for par in range(2):
                for n in range(3):
                    total = total + ww[(o * 3 + n) * 2 + par] * faces[par][n]
            tpad[o, pl.ds(8, 48), :] = total
        total = tpad[0, pl.ds(10, 48), :]
        for o in range(1, 5):
            total = total + tpad[o, pl.ds(10 - o, 48), :]
        sin[2 + k] = total
        sins[k] = total[8:40]

    def face_row(src, dst, a_ref, b_ref, cut_left, cut_right, x):
        base = at_row(x, 8)
        cur = src[pl.ds(base, 8), :]
        keep_left = jnp.where(cut_left(x), 0.0, 1.0).astype(F32)
        keep_right = jnp.where(cut_right(x), 0.0, 1.0).astype(F32)
        summed = src[pl.ds(base - 8, 8), :] * keep_left + src[pl.ds(base + 8, 8), :] * keep_right
        summed = summed + ysum(cur) + zsum(cur)
        dst[pl.ds(base, 8), :] = b_ref[pl.ds(base, 8), :] + a_ref[pl.ds(base, 8), :] * summed

    at_first, at_last = d == 0, d == n_dom - 1

    def cuts(width):
        def cut_left(x):
            return ((x == width) & at_first) | ((x == 2 * width) & at_last)

        def cut_right(x):
            return ((x == width - 1) & at_first) | ((x == 2 * width - 1) & at_last)

        return cut_left, cut_right

    fcut, scut = cuts(FX), cuts(SX)
    fluid_span = (((13, 83), (14, 82)), ((19, 77), (20, 76)), ((25, 71), (26, 70)))
    solid_span = (((6, 42), (7, 41)), ((9, 39), (10, 38)), ((12, 36), (13, 35)))
    fluid_refs = (xf0, xf0, xf2)
    fluid_out = (xf0, xf2, xf0)
    for k in range(4):
        fluid_ref = (xf0, xf0, xf2, xf0)[k]
        project_fluid(xs0, k)
        project_solid(fluid_ref, k)
        if k == 3:
            break
        for par in range(2):
            xb[pl.ds(par * 8, 48, stride=16), :] = fin[xb0[par]] + fin[4 + 2 * k + par]
        xsb[srows, :] = sin[0] + sin[1] * sin[2 + k]
        for n in range(2):
            lo, hi = fluid_span[k][n]
            src, dst = (fluid_refs[k], xf1) if n == 0 else (xf1, fluid_out[k])
            rows_loop(lo, hi, 8, lambda x: face_row(src, dst, xa, xb, *fcut, x))
            lo, hi = solid_span[k][n]
            src, dst = (xs0, xs1) if n == 0 else (xs1, xs0)
            rows_loop(lo, hi, 8, lambda x: face_row(src, dst, xsa, xsb, *scut, x))
    recv["sinr"] = send(sins, sinr, 22, (gp, d))

    recv["bhlr"].wait_recv()
    recv["bhrr"].wait_recv()
    for ref, first_row, mask, film_at in ((bhlr, 0, ml, 28), (bhrr, 36, mr, 64)):
        for i in range(4):
            p[pl.ds((first_row + i) * FY, FY), :] = to_f32(ref[pl.ds(i * FY, FY), :]) * mask
        skip = 1 if first_row == 0 else 0
        for i in range(3):
            row = first_row + skip + i
            a[pl.ds(row * FY, FY), :] = to_f32(ref[pl.ds((4 + i) * FY, FY), :]) * mask
        for i in range(3):
            row = first_row + skip + i
            film = fxx[pl.ds(film_at + skip + i, 1), :]
            r0, s0 = a[pl.ds(row * FY, 1), :], p[pl.ds(row * FY, 1), :]
            a0, b0, _ = film_coef(r0, s0, film)
            coef(p, a, a, b, row * FY, FY)
            a[pl.ds(row * FY, 1), :] = a0
            b[pl.ds(row * FY, 1), :] = b0
    edges((None,) * 4)
    mhl[...] = p[pl.ds(4 * FY, 4 * FY), :].astype(BF16)
    mhr[...] = p[pl.ds(32 * FY, 4 * FY), :].astype(BF16)
    recv["mhrr"] = send(mhl, mhrr, 20, (g, dm))
    recv["mhlr"] = send(mhr, mhlr, 21, (g, dp))

    wide = lax.broadcasted_iota(jnp.int32, (20, FZ), 0)
    inside = jnp.where(wide < 2, ml, jnp.where(wide >= 18, mr, 1.0))
    for v in range(2):
        for i in range(1, 39):
            bt[pl.ds(v * 320 + i * 8, 8), :] = b[pl.ds(i * FY, 8), :]
        for par in range(2):
            rows = pl.ds(v * 320 + par * 8, 20, stride=16)
            bt[rows, :] = bt[rows, :] + fin[4 + 2 * (2 + v) + par][14:34] * inside

    def patch(i, mask):
        low = lax.broadcasted_iota(jnp.int32, (8, FZ), 0) < 4
        fresh = xf2[pl.ds((28 + i) * 8, 8), :]
        if mask is not None:
            fresh = fresh * mask
        p[pl.ds(i * FY, 8), :] = jnp.where(low, fresh, p[pl.ds(i * FY, 8), :])

    for i in range(4, 36):
        patch(i, None)
    second = (0, 0, 1, 1)
    interior(second)
    out_mid = pltpu.make_async_copy(
        p.at[pl.ds(8 * FY, 24 * FY)], fo.at[pl.ds(4 * FY, 24 * FY)], load_sem.at[19]
    )
    out_mid.start()

    for name in ("scbl", "scbr", "shlr", "shrr", "sinr"):
        recv[name].wait_recv()
    for f, ref in ((0, sp), (1, sa)):
        ref[pl.ds(0, 8 * SY), :] = to_f32(shlr[f]) * ml
        ref[pl.ds(24 * SY, 8 * SY), :] = to_f32(shrr[f]) * mr
    fsx[pl.ds(0, 8), :] = scbl[pl.ds(8, 8), :] * ml
    fsx[pl.ds(8, SX), :] = scv[...]
    fsx[pl.ds(24, 8), :] = scbr[pl.ds(0, 8), :] * mr
    last_rows = pl.ds(SY - 1, 32, stride=SY)
    a0, b0, c0 = film_coef(sa[last_rows, :], sp[last_rows, :], fsx[...])
    rows_loop(0, 8, 2, lambda x: coef(sp, sa, sa, sbb, at_row(x, 96), 96))
    sa[last_rows, :] = a0
    sbb[last_rows, :] = b0
    for k in range(4):
        for i in range(32):
            sbt[pl.ds(k * 256 + i * 8, 8), :] = sbb[pl.ds(i * SY + 16, 8), :]
        sbt[pl.ds(k * 256 + 7, 32, stride=8), :] = b0 + c0 * sinr[k]

    def solid_row(src, dst, variant, x):
        base = at_row(x, SY)
        cur = src[pl.ds(base, SY), :]
        summed = src[pl.ds(base - SY, SY), :] + src[pl.ds(base + SY, SY), :]
        summed = summed + ysum(cur) + zsum(cur)
        high = sbt[pl.ds(variant * 256 + at_row(x, 8), 8), :]
        fixed = jnp.concatenate([sbb[pl.ds(base, 16), :], high], axis=0)
        dst[pl.ds(base, SY), :] = fixed + sa[pl.ds(base, SY), :] * summed

    for m in range(8):
        src, dst = (sp, sq) if m % 2 == 0 else (sq, sp)
        rows_loop(1 + m, 31 - m, 8, lambda x: solid_row(src, dst, m // 2, x))
    out_solid = pltpu.make_async_copy(sp.at[pl.ds(8 * SY, SX * SY)], so, load_sem.at[20])
    out_solid.start()

    recv["mhlr"].wait_recv()
    recv["mhrr"].wait_recv()
    p[pl.ds(0, 4 * FY), :] = to_f32(mhlr[...]) * ml
    p[pl.ds(36 * FY, 4 * FY), :] = to_f32(mhrr[...]) * mr
    for i in range(4):
        patch(i, ml)
        patch(36 + i, mr)
    edges(second)
    outs = []
    for n, i in enumerate((4, 32)):
        copy = pltpu.make_async_copy(
            p.at[pl.ds(i * FY, 4 * FY)], fo.at[pl.ds((i - 4) * FY, 4 * FY)], load_sem.at[21 + n]
        )
        copy.start()
        outs.append(copy)
    for copy in sends:
        copy.wait_send()
    for copy in (out_mid, out_solid, *outs):
        copy.wait()


def vm(*shape, dtype=F32):
    return pltpu.VMEM(shape, dtype)


SCRATCH = [
    *(vm(40 * FY, FZ) for _ in range(4)), vm(2 * 320, FZ),
    *(vm(32 * SY, FZ) for _ in range(4)), vm(4 * 256, FZ),
    vm(2 * SEG * FZ, FZ, dtype=BF16), vm(2 * SEG * 8, FZ),
    *(vm(96 * 8, FZ) for _ in range(6)), *(vm(48 * 8, FZ) for _ in range(5)),
    vm(6, 3 * SEG, FZ), vm(30, 48, FZ), vm(30, 48, FZ), vm(3, 64, FZ), vm(5, 64, FZ),
    vm(12, 48, FZ), vm(6, 48, FZ), vm(4, 32, FZ), vm(96, FZ), vm(32, FZ),
    vm(3 * SEG, FZ, dtype=jnp.int32),
    vm(FX, FZ), vm(SX, FZ), vm(1, FZ, dtype=jnp.int32),
    vm(2, 256, FZ, dtype=BF16), vm(2, 128, FZ, dtype=BF16), vm(6, SEG, FZ, dtype=BF16),
    vm(7 * FY, FZ, dtype=BF16), vm(7 * FY, FZ, dtype=BF16),
    vm(2, 8 * SY, FZ, dtype=BF16), vm(2, 8 * SY, FZ, dtype=BF16),
    vm(4 * FY, FZ, dtype=BF16), vm(4 * FY, FZ, dtype=BF16),
    vm(2, 192, FZ, dtype=BF16), vm(2, 192, FZ, dtype=BF16), vm(FX, FZ), vm(FX, FZ),
    vm(1, FZ, dtype=jnp.int32), vm(1, FZ, dtype=jnp.int32),
    *(vm(2, 128, FZ, dtype=BF16) for _ in range(3)), *(vm(SX, FZ) for _ in range(5)),
    vm(6, 80, FZ, dtype=BF16), vm(6, 80, FZ, dtype=BF16),
    vm(7 * FY, FZ, dtype=BF16), vm(7 * FY, FZ, dtype=BF16),
    vm(2, 8 * SY, FZ, dtype=BF16), vm(2, 8 * SY, FZ, dtype=BF16),
    vm(4 * FY, FZ, dtype=BF16), vm(4 * FY, FZ, dtype=BF16), vm(4, 32, FZ),
    pltpu.SemaphoreType.DMA((24,)), pltpu.SemaphoreType.DMA((23,)), pltpu.SemaphoreType.DMA((23,)),
]


def solution(mesh):
    n_grp, n_dom = mesh.shape["grp"], mesh.shape["dom"]

    def local(fs, fr, fc, ss, sr, sc, sb, ts, tf):
        fo, so = pl.pallas_call(
            lambda *refs: kernel(n_grp, n_dom, *refs),
            out_shape=(
                jax.ShapeDtypeStruct((FX * FY, FZ), F32),
                jax.ShapeDtypeStruct((SX * SY, FZ), F32),
            ),
            in_specs=[pl.BlockSpec(memory_space=pl.ANY)] * 9,
            out_specs=[pl.BlockSpec(memory_space=pl.ANY)] * 2,
            scratch_shapes=SCRATCH,
            compiler_params=pltpu.CompilerParams(
                collective_id=0, has_side_effects=True, vmem_limit_bytes=56 * 1024 * 1024
            ),
            name="coupled",
        )(
            fs.reshape(FX * FY, FZ), fr.reshape(FX * FY, FZ), fc.reshape(FX, FZ),
            ss.reshape(SX * SY, FZ), sr.reshape(SX * SY, FZ), sc.reshape(SX, FZ),
            jnp.pad(sb, (0, FZ - SEG)).reshape(1, FZ),
            ts.reshape(SEG * FZ, FZ), tf.reshape(SEG * FZ, FZ),
        )
        return fo.reshape(1, FX, FY, FZ), so.reshape(1, SX, SY, FZ)

    cells = P("grp", "dom", None, None)
    faces = P("grp", "dom", None)
    split = P(("grp", "dom"))
    mats = P(("grp", "dom"), None, None)
    return jax.shard_map(
        local,
        mesh=mesh,
        in_specs=(cells, cells, faces, cells, cells, faces, split, mats, mats),
        out_specs=(cells, cells),
        check_vma=False,
    )
```

profile of v0, /device:TPU:0, one launch (start us, length us, event | category | flops | bytes accessed | tf_op | source)
XLA Modules:
  0.0 38.4 jit_solution(11276506577708168802)
XLA Ops:
  0.6 1.2 %pad_bitcast_fusion.refs_6_ = s32[1,128]{1,0:T(1,128)} fusion(s32[96]{0:T(128)} %param.15), kind=kLoop, calls=%fused_computation | loop fusion | bytes 896 | tf_op jit(solution)/shard_map/reshape | solution.py:524
  1.8 33.2 %coupled.1 = (f32[3072,128]{1,0:T(8,128)}, f32[384,128]{1,0:T(8,128)}) custom-call(f32[3072,128]{1,0:T(8,128)} %bitcast.15, f32[3072,128]{1,0:T(8,128)} %bitcast.16, f32[32,128]{1,0:T(8,128)} %bitcast.20, f32[384,128]{1,0:T(8,128)} %bitcast.18, f32[384,128]{1,0:T(8,128)} %bitcast.19, f32[16,128]{1,0:T(8,128)} %bitcast.21, s32[1,128]{1,0:T(1,128)} %pad_bitcast_fusion.refs_6_, ...), custom_call_target="tpu_custom_call" | custom-call | tf_op jit(solution)/shard_map/coupled/pallas_call | solution.py:508
  35.0 0.0 copy-start
  35.0 2.7 %copy.13 = f32[1,32,96,128]{3,2,1,0:T(8,128)} copy(f32[1,32,96,128]{3,2,1,0:T(8,128)} %bitcast.14) | data formatting | bytes 3145728
  37.7 0.0 copy-done
  37.7 0.7 %copy.14 = f32[1,16,24,128]{3,2,1,0:T(8,128)} copy(f32[1,16,24,128]{3,2,1,0:T(8,128)S(1)} %bitcast.17) | data formatting | bytes 393216
Async XLA Ops:
  35.0 2.7 %copy-start = (f32[384,128]{1,0:T(8,128)S(1)}, f32[384,128]{1,0:T(8,128)}, u32[]{:S(2)}) copy-start(f32[384,128]{1,0:T(8,128)} %get-tuple-element.5) | copy-start | bytes 589828
where the time goes:
time: 38.5 us; the launch traced here: 38.4 us
  Pallas kernels  33.2 us (86%)
  local copies, waits for them, and re-layouts  4.55 us (12%)
  between operations  0.65 us (2%)
    pallas_call x1, Pallas kernels, local(): pl.pallas_call(lambda *refs: kernel(n_grp, n_dom, *refs), out_shape=(jax....  33.2 us
    unnamed x4, local copies, waits for them, and re-layouts  3.38 us
    reshape x1, local copies, waits for them, and re-layouts, local(): jnp.pad(sb, (0, FZ - SEG)).reshape(1, FZ)  1.17 us

commit v1 on v0

--- a/solution.py
+++ b/solution.py
@@ -25,6 +25,17 @@
     )
 
 
+def split_terms(v):
+    head = v.astype(BF16)
+    return jnp.concatenate([head, (v - head.astype(F32)).astype(BF16)], axis=1)
+
+
+def zsum_by_product(values, tt):
+    return jnp.dot(
+        jnp.concatenate([split_terms(v) for v in values], axis=0), tt, preferred_element_type=F32
+    )
+
+
 def ysum(v):
     zero = jnp.zeros((1, FZ), F32)
     return jnp.concatenate([zero, v[:-1]], axis=0) + jnp.concatenate([v[1:], zero], axis=0)
@@ -47,6 +58,48 @@
 
 def at_row(x, pitch):
     return x * pitch if isinstance(x, int) else pl.multiple_of(x * pitch, 8)
+
+
+def ysum_tile(ref, at, tile, tiles, cur):
+    zero = jnp.zeros((1, FZ), F32)
+    if 0 < tile < tiles - 1 and tile % 2 == 0:
+        return ref[pl.ds(at - 1, 8), :] + ref[pl.ds(at + 1, 8), :]
+    low = zero if tile == 0 else ref[pl.ds(at - 1, 1), :]
+    high = zero if tile == tiles - 1 else ref[pl.ds(at + 8, 1), :]
+    return jnp.concatenate([low, cur[:-1]], axis=0) + jnp.concatenate([cur[1:], high], axis=0)
+
+
+def sweep_rows(groups, tiles, rolled, tt, coef_a, fixed):
+    products = []
+    for group in groups:
+        halves = [group[: len(group) // 2], group[len(group) // 2 :]]
+        for part in halves if len(group) > 1 and tiles > rolled else [group]:
+            if tiles == rolled:
+                products.extend([None] * len(part))
+                continue
+            height = 8 * (tiles - rolled)
+            total = zsum_by_product(
+                [ref[pl.ds(at + 8 * rolled, height), :] for _, (ref, at), _, _ in part], tt
+            )
+            products.extend(total[n * height : (n + 1) * height] for n in range(len(part)))
+    for tile in range(tiles):
+        n = 0
+        for group in groups:
+            cur = None
+            for left, row, right, target in group:
+                here = row[1] + 8 * tile
+                before = cur if cur is not None else left[0][pl.ds(left[1] + 8 * tile, 8), :]
+                cur = after if cur is not None else row[0][pl.ds(here, 8), :]
+                after = right[0][pl.ds(right[1] + 8 * tile, 8), :]
+                summed = (before + after) + ysum_tile(row[0], here, tile, tiles, cur)
+                if tile < rolled:
+                    summed = summed + zsum(cur)
+                else:
+                    summed = summed + products[n][8 * (tile - rolled) : 8 * (tile - rolled + 1)]
+                target[0][pl.ds(target[1] + 8 * tile, 8), :] = (
+                    fixed(n, tile) + coef_a(n, tile) * summed
+                )
+                n += 1
 
 
 def to_f32(v):
@@ -64,7 +117,7 @@
     p, q, a, b, bt, sp, sq, sa, sbb, sbt,
     mt, yy, xf0, xf1, xf2, xr, xa, xb, xs0, xs1, xsr, xsa, xsb,
     dx, vv, ww, pad, tpad, fin, sin, sins, fxx, fsx, xoff,
-    fcv, scv, sbv,
+    fcv, scv, sbv, tt,
     ifs, is_, wb, bhl, bhr, shl, shr, mhl, mhr,
     rfl, rfr, fcl, fcr, sbl, sbr, rso, rsr, rsl, sco, scr, scl, scbr, scbl,
     wr, wl, bhrr, bhlr, shrr, shlr, mhrr, mhlr, sinr,
@@ -97,13 +150,15 @@
     load("sb", sb, sbv, 6)
     chunk = GROUP * FZ
     for t, src in ((0, ts), (1, tf)):
-        for c in range(SEG // GROUP):
+        for c in (0, 3, 1, 4, 2, 5):
             load(
                 ("m", t, c), src.at[pl.ds(c * chunk, chunk)],
                 mt.at[pl.ds((t * SEG * FZ) + c * chunk, chunk)], 7 + t * 6 + c,
             )
 
     sends = []
+    apart = (lax.broadcasted_iota(jnp.int32, (2 * FZ, FZ), 0) & (FZ - 1)) - lane_iota((2 * FZ, FZ))
+    tt[...] = jnp.where((apart == 1) | (apart == -1), 1.0, 0.0).astype(BF16)
 
     def send(src, dst, index, peer):
         copy = pltpu.make_async_remote_copy(
@@ -154,29 +209,34 @@
     recv["scbr"] = send(scv, scbr, 12, (g, dm))
     recv["scbl"] = send(scv, scbl, 13, (g, dp))
 
-    prow = lax.broadcasted_iota(jnp.int32, (8, FZ), 0)
-    pcol = lane_iota((8, FZ))
-    probe = jnp.where(lax.rem(pcol, 3) == prow, 1.0, 0.0).astype(BF16)
+    prow = lax.broadcasted_iota(jnp.int32, (8, 2 * FZ), 0)
+    pcol = lane_iota((8, 2 * FZ))
+    wanted = jnp.where(pcol < FZ, lax.rem(pcol, 3), lax.rem(pcol - FZ, 3) + 3)
+    probe = jnp.where(wanted == prow, 1.0, 0.0).astype(BF16)
+    phase = lax.rem(lane_iota((24, FZ)), 3)
     for t in range(2):
-        for c in range(SEG // GROUP):
+        for c in range(3):
             loads[("m", t, c)].wait()
-            for s in range(GROUP):
-                at = t * SEG + c * GROUP + s
-                yy[pl.ds(at * 8, 8), :] = jnp.dot(
-                    probe, mt[pl.ds(at * FZ, FZ), :], preferred_element_type=F32
+            loads[("m", t, 3 + c)].wait()
+            for v in range(8 * c, 8 * c + 8):
+                at = (t * SEG + 2 * v) * FZ
+                four = jnp.concatenate(
+                    [mt[pl.ds(at, 2 * FZ), :], mt[pl.ds(at + 48 * FZ, 2 * FZ), :]], axis=1
                 )
-        y3 = [yy[pl.ds(t * SEG * 8 + c, SEG, stride=8), :] for c in range(3)]
-        phase = lax.rem(lane_iota((SEG, FZ)), 3)
-        for k, shift in enumerate((0, 2, 1)):
-            picked = y3[(0 + shift) % 3]
-            picked = jnp.where(phase == 1, y3[(1 + shift) % 3], picked)
-            picked = jnp.where(phase == 2, y3[(2 + shift) % 3], picked)
-            if k == 1:
-                picked = jnp.where(lane_iota((SEG, FZ)) == 0, 0.0, picked)
-            if k == 2:
-                picked = jnp.where(lane_iota((SEG, FZ)) == FZ - 1, 0.0, picked)
-            dx[3 * t + k, pl.ds(SEG, SEG), :] = picked
-            wb[3 * t + k] = picked.astype(BF16)
+                found = jnp.dot(probe, four, preferred_element_type=F32)
+                yy[pl.ds(t * 384 + v * 8, 8), :] = found[:, :FZ]
+                yy[pl.ds(t * 384 + 192 + v * 8, 8), :] = found[:, FZ:]
+        for h in range(2):
+            for e in range(2):
+                y3 = [
+                    yy[pl.ds(t * 384 + h * 192 + 3 * e + c, 24, stride=8), :] for c in range(3)
+                ]
+                for k, shift in enumerate((0, 2, 1)):
+                    picked = jnp.where(phase == 1, y3[(1 + shift) % 3], y3[shift])
+                    picked = jnp.where(phase == 2, y3[(2 + shift) % 3], picked)
+                    dx[3 * t + k, pl.ds(SEG + 48 * h + e, 24, stride=2), :] = picked
+        for k in range(3):
+            wb[3 * t + k] = dx[3 * t + k, pl.ds(SEG, SEG), :].astype(BF16)
     recv["wr"] = send(wb.at[:, pl.ds(0, 80)], wr, 14, (g, dm))
     recv["wl"] = send(wb.at[:, pl.ds(16, 80)], wl, 15, (g, dp))
 
@@ -207,31 +267,40 @@
     a[own_rows, :] = a0
     b[own_rows, :] = b0
 
-    def fluid_row(src, dst, variant, x):
-        base = at_row(x, FY)
-        cur = src[pl.ds(base, FY), :]
-        summed = src[pl.ds(base - FY, FY), :] + src[pl.ds(base + FY, FY), :]
-        summed = summed + ysum(cur) + zsum(cur)
-        if variant is None:
-            fixed = b[pl.ds(base, FY), :]
-        else:
-            low = bt[pl.ds(variant * 320 + at_row(x, 8), 8), :]
-            fixed = jnp.concatenate([low, b[pl.ds(base + 8, FY - 8), :]], axis=0)
-        dst[pl.ds(base, FY), :] = fixed + a[pl.ds(base, FY), :] * summed
+    def fluid_sweep(src, dst, variant, spans):
+        groups, bases, rows = [], [], []
+        for x0, count in spans:
+            group = []
+            for n in range(count):
+                base = x0 * FY + n * FY if isinstance(x0, int) else pl.multiple_of(x0 * FY, 8) + n * FY
+                bases.append(base)
+                rows.append(x0 + n)
+                group.append(((src, base - FY), (src, base), (src, base + FY), (dst, base)))
+            groups.append(group)
+
+        def fixed(n, tile):
+            if tile == 0 and variant is not None:
+                return bt[pl.ds(variant * 320 + at_row(rows[n], 8), 8), :]
+            return b[pl.ds(bases[n] + 8 * tile, 8), :]
+
+        sweep_rows(
+            groups, 12, 6, tt[...], lambda n, tile: a[pl.ds(bases[n] + 8 * tile, 8), :], fixed
+        )
 
     def interior(variants):
-        for m in range(4):
+        for m, block in enumerate((10, 7, 13, 8)):
             src, dst = (p, q) if m % 2 == 0 else (q, p)
-            rows_loop(
-                5 + m, 35 - m, 8, lambda x: fluid_row(src, dst, variants[m], x)
-            )
+
+            def step(i, carry):
+                fluid_sweep(src, dst, variants[m], ((5 + m + i * block, block),))
+                return carry
+
+            lax.fori_loop(0, (30 - 2 * m) // block, step, 0)
 
     def edges(variants):
         for m in range(4):
             src, dst = (p, q) if m % 2 == 0 else (q, p)
-            for x0 in (1 + m, 35 - m):
-                for x in range(x0, x0 + 4):
-                    fluid_row(src, dst, variants[m], x)
+            fluid_sweep(src, dst, variants[m], ((1 + m, 4), (35 - m, 4)))
 
     interior((None,) * 4)
 
@@ -249,8 +318,8 @@
     xc = []
     xb0 = []
     for par in range(2):
-        rows = pl.ds(par * 8, 48, stride=16)
-        film = fxx[pl.ds(par, 48, stride=2), :]
+        rows = pl.ds(64 + par * 8, 40, stride=16)
+        film = fxx[pl.ds(8 + par, 40, stride=2), :]
         a0, b0, c0 = film_coef(xr[rows, :], xf0[rows, :], film)
         xa[rows, :] = a0
         fin[par] = b0
@@ -265,8 +334,8 @@
         ref[pl.ds(128, 128), :] = to_f32(rso[f])
         ref[pl.ds(256, 128), :] = to_f32(rsr[f])
     rows_loop(0, 6, 2, lambda x: coef(xs0, xsr, xsa, xsb, at_row(x, 64), 64))
-    srows = pl.ds(7, 48, stride=8)
-    film = jnp.concatenate([scl[...], sco[...], scr[...]], axis=0)
+    srows = pl.ds(32 + 7, 40, stride=8)
+    film = jnp.concatenate([scl[...], sco[...], scr[...]], axis=0)[4:44]
     a0, b0, c0 = film_coef(xsr[srows, :], xs0[srows, :], film)
     xsa[srows, :] = a0
     sin[0] = b0
@@ -282,15 +351,15 @@
         xoff[pl.ds(n * SEG, SEG), :] = spread[:SEG].astype(jnp.int32)
     first = SX * (d + n_dom - 1) - 2
     zone = SX * n_dom
-    half = lax.broadcasted_iota(jnp.int32, (48, FZ), 0) + first
+    half = lax.broadcasted_iota(jnp.int32, (40, FZ), 0) + (first + 4)
     for par in range(2):
         offs = [
-            lax.rem(xoff[pl.ds(3 * par + j, 48, stride=6), :] - half + 3 * zone, zone)
+            lax.rem(xoff[pl.ds(24 + 3 * par + j, 40, stride=6), :] - half + 3 * zone, zone)
             for j in range(3)
         ]
         for t in range(2):
             for k in range(3):
-                diag = [dx[3 * t + k, pl.ds(3 * par + j, 48, stride=6), :] for j in range(3)]
+                diag = [dx[3 * t + k, pl.ds(24 + 3 * par + j, 40, stride=6), :] for j in range(3)]
                 for o in range(5):
                     total = jnp.where(offs[0] == o, diag[0], 0.0)
                     total = total + jnp.where(offs[1] == o, diag[1], 0.0)
@@ -306,49 +375,58 @@
 
     def project_fluid(solid_ref, k):
         for n, v in enumerate(shifts(rounded(solid_ref[srows, :]))):
-            pad[n, pl.ds(8, 48), :] = v
+            pad[n, pl.ds(8, 40), :] = v
         for par in range(2):
-            total = jnp.zeros((48, FZ), F32)
+            total = jnp.zeros((40, FZ), F32)
             for o in range(5):
                 for n in range(3):
-                    total = total + vv[(o * 3 + n) * 2 + par] * pad[n, pl.ds(6 + o, 48), :]
+                    total = total + vv[(o * 3 + n) * 2 + par] * pad[n, pl.ds(6 + o, 40), :]
             fin[4 + 2 * k + par] = total
 
     def project_solid(fluid_ref, k):
-        faces = [shifts(rounded(fluid_ref[pl.ds(par * 8, 48, stride=16), :])) for par in range(2)]
+        faces = [
+            shifts(rounded(fluid_ref[pl.ds(64 + par * 8, 40, stride=16), :])) for par in range(2)
+        ]
         for o in range(5):
-            total = jnp.zeros((48, FZ), F32)
+            total = jnp.zeros((40, FZ), F32)
             for par in range(2):
                 for n in range(3):
                     total = total + ww[(o * 3 + n) * 2 + par] * faces[par][n]
-            tpad[o, pl.ds(8, 48), :] = total
-        total = tpad[0, pl.ds(10, 48), :]
+            tpad[o, pl.ds(8, 40), :] = total
+        total = tpad[0, pl.ds(10, 40), :]
         for o in range(1, 5):
-            total = total + tpad[o, pl.ds(10 - o, 48), :]
+            total = total + tpad[o, pl.ds(10 - o, 40), :]
         sin[2 + k] = total
-        sins[k] = total[8:40]
-
-    def face_row(src, dst, a_ref, b_ref, cut_left, cut_right, x):
-        base = at_row(x, 8)
-        cur = src[pl.ds(base, 8), :]
-        keep_left = jnp.where(cut_left(x), 0.0, 1.0).astype(F32)
-        keep_right = jnp.where(cut_right(x), 0.0, 1.0).astype(F32)
-        summed = src[pl.ds(base - 8, 8), :] * keep_left + src[pl.ds(base + 8, 8), :] * keep_right
-        summed = summed + ysum(cur) + zsum(cur)
-        dst[pl.ds(base, 8), :] = b_ref[pl.ds(base, 8), :] + a_ref[pl.ds(base, 8), :] * summed
-
-    at_first, at_last = d == 0, d == n_dom - 1
-
-    def cuts(width):
-        def cut_left(x):
-            return ((x == width) & at_first) | ((x == 2 * width) & at_last)
-
-        def cut_right(x):
-            return ((x == width - 1) & at_first) | ((x == 2 * width - 1) & at_last)
-
-        return cut_left, cut_right
-
-    fcut, scut = cuts(FX), cuts(SX)
+        sins[k] = total[4:36]
+
+    def face_sweep(src, dst, a_ref, b_ref, width, lo, hi):
+        count = hi - lo
+        by_rolls = count - 2 * (count // 4)
+
+        def beside(step, first):
+            pieces, x = [], lo + step
+            for cut, keep in ((width, keep_first), (2 * width, keep_last)):
+                row = cut - 1 if first else cut
+                if x < row:
+                    pieces.append(src[pl.ds(x * 8, (row - x) * 8), :])
+                pieces.append(src[pl.ds(row * 8, 8), :] * keep)
+                x = row + 1
+            if x < hi + step:
+                pieces.append(src[pl.ds(x * 8, (hi + step - x) * 8), :])
+            return jnp.concatenate(pieces, axis=0)
+
+        cur = src[pl.ds(lo * 8, count * 8), :]
+        sub = lax.broadcasted_iota(jnp.int32, (count * 8, FZ), 0) & 7
+        above = jnp.where(sub == 0, 0.0, src[pl.ds(lo * 8 - 1, count * 8), :])
+        below = jnp.where(sub == 7, 0.0, src[pl.ds(lo * 8 + 1, count * 8), :])
+        along = jnp.concatenate(
+            [zsum(cur[: by_rolls * 8]), zsum_by_product([cur[by_rolls * 8 :]], tt[...])], axis=0
+        )
+        summed = (beside(-1, True) + beside(1, False)) + (above + below) + along
+        span = pl.ds(lo * 8, count * 8)
+        dst[span, :] = b_ref[span, :] + a_ref[span, :] * summed
+
+    keep_first, keep_last = ml, mr
     fluid_span = (((13, 83), (14, 82)), ((19, 77), (20, 76)), ((25, 71), (26, 70)))
     solid_span = (((6, 42), (7, 41)), ((9, 39), (10, 38)), ((12, 36), (13, 35)))
     fluid_refs = (xf0, xf0, xf2)
@@ -360,15 +438,15 @@
         if k == 3:
             break
         for par in range(2):
-            xb[pl.ds(par * 8, 48, stride=16), :] = fin[xb0[par]] + fin[4 + 2 * k + par]
+            xb[pl.ds(64 + par * 8, 40, stride=16), :] = fin[xb0[par]] + fin[4 + 2 * k + par]
         xsb[srows, :] = sin[0] + sin[1] * sin[2 + k]
         for n in range(2):
             lo, hi = fluid_span[k][n]
             src, dst = (fluid_refs[k], xf1) if n == 0 else (xf1, fluid_out[k])
-            rows_loop(lo, hi, 8, lambda x: face_row(src, dst, xa, xb, *fcut, x))
+            face_sweep(src, dst, xa, xb, FX, lo, hi)
             lo, hi = solid_span[k][n]
             src, dst = (xs0, xs1) if n == 0 else (xs1, xs0)
-            rows_loop(lo, hi, 8, lambda x: face_row(src, dst, xsa, xsb, *scut, x))
+            face_sweep(src, dst, xsa, xsb, SX, lo, hi)
     recv["sinr"] = send(sins, sinr, 22, (gp, d))
 
     recv["bhlr"].wait_recv()
@@ -401,7 +479,7 @@
             bt[pl.ds(v * 320 + i * 8, 8), :] = b[pl.ds(i * FY, 8), :]
         for par in range(2):
             rows = pl.ds(v * 320 + par * 8, 20, stride=16)
-            bt[rows, :] = bt[rows, :] + fin[4 + 2 * (2 + v) + par][14:34] * inside
+            bt[rows, :] = bt[rows, :] + fin[4 + 2 * (2 + v) + par][10:30] * inside
 
     def patch(i, mask):
         low = lax.broadcasted_iota(jnp.int32, (8, FZ), 0) < 4
@@ -437,18 +515,19 @@
             sbt[pl.ds(k * 256 + i * 8, 8), :] = sbb[pl.ds(i * SY + 16, 8), :]
         sbt[pl.ds(k * 256 + 7, 32, stride=8), :] = b0 + c0 * sinr[k]
 
-    def solid_row(src, dst, variant, x):
-        base = at_row(x, SY)
-        cur = src[pl.ds(base, SY), :]
-        summed = src[pl.ds(base - SY, SY), :] + src[pl.ds(base + SY, SY), :]
-        summed = summed + ysum(cur) + zsum(cur)
-        high = sbt[pl.ds(variant * 256 + at_row(x, 8), 8), :]
-        fixed = jnp.concatenate([sbb[pl.ds(base, 16), :], high], axis=0)
-        dst[pl.ds(base, SY), :] = fixed + sa[pl.ds(base, SY), :] * summed
-
     for m in range(8):
         src, dst = (sp, sq) if m % 2 == 0 else (sq, sp)
-        rows_loop(1 + m, 31 - m, 8, lambda x: solid_row(src, dst, m // 2, x))
+        rows = range(1 + m, 31 - m)
+
+        def fixed(n, tile):
+            if tile == 2:
+                return sbt[pl.ds((m // 2) * 256 + rows[n] * 8, 8), :]
+            return sbb[pl.ds(rows[n] * SY + 8 * tile, 8), :]
+
+        sweep_rows(
+            [[((src, (x - 1) * SY), (src, x * SY), (src, (x + 1) * SY), (dst, x * SY)) for x in rows]],
+            3, 1, tt[...], lambda n, tile: sa[pl.ds(rows[n] * SY + 8 * tile, 8), :], fixed,
+        )
     out_solid = pltpu.make_async_copy(sp.at[pl.ds(8 * SY, SX * SY)], so, load_sem.at[20])
     out_solid.start()
 
@@ -482,10 +561,10 @@
     *(vm(32 * SY, FZ) for _ in range(4)), vm(4 * 256, FZ),
     vm(2 * SEG * FZ, FZ, dtype=BF16), vm(2 * SEG * 8, FZ),
     *(vm(96 * 8, FZ) for _ in range(6)), *(vm(48 * 8, FZ) for _ in range(5)),
-    vm(6, 3 * SEG, FZ), vm(30, 48, FZ), vm(30, 48, FZ), vm(3, 64, FZ), vm(5, 64, FZ),
-    vm(12, 48, FZ), vm(6, 48, FZ), vm(4, 32, FZ), vm(96, FZ), vm(32, FZ),
+    vm(6, 3 * SEG, FZ), vm(30, 40, FZ), vm(30, 40, FZ), vm(3, 64, FZ), vm(5, 64, FZ),
+    vm(12, 40, FZ), vm(6, 40, FZ), vm(4, 32, FZ), vm(96, FZ), vm(32, FZ),
     vm(3 * SEG, FZ, dtype=jnp.int32),
-    vm(FX, FZ), vm(SX, FZ), vm(1, FZ, dtype=jnp.int32),
+    vm(FX, FZ), vm(SX, FZ), vm(1, FZ, dtype=jnp.int32), vm(2 * FZ, FZ, dtype=BF16),
     vm(2, 256, FZ, dtype=BF16), vm(2, 128, FZ, dtype=BF16), vm(6, SEG, FZ, dtype=BF16),
     vm(7 * FY, FZ, dtype=BF16), vm(7 * FY, FZ, dtype=BF16),
     vm(2, 8 * SY, FZ, dtype=BF16), vm(2, 8 * SY, FZ, dtype=BF16),

time: 38.5 us -> 30.8 us (0.80)
  Pallas kernels: 33.2 us -> 25.5 us
    pallas_call x1, Pallas kernels: 33.2 us -> 25.5 us  [local(): pl.pallas_call(lambda *refs: kernel(n_grp, n_dom, *refs), out_shape=(jax....]
where the time goes in v1:
time: 30.8 us; the launch traced here: 30.7 us
  Pallas kernels  25.5 us (83%)
  local copies, waits for them, and re-layouts  4.55 us (15%)
  between operations  0.65 us (2%)
    pallas_call x1, Pallas kernels, local(): pl.pallas_call(lambda *refs: kernel(n_grp, n_dom, *refs), out_shape=(jax....  25.5 us
    unnamed x4, local copies, waits for them, and re-layouts  3.38 us
    reshape x1, local copies, waits for them, and re-layouts, local(): jnp.pad(sb, (0, FZ - SEG)).reshape(1, FZ)  1.17 us

profile of v1, /device:TPU:0, one launch (start us, length us, event | category | flops | bytes accessed | tf_op | source)
XLA Modules:
  0.0 30.7 jit_solution(12751739368490079592)
XLA Ops:
  0.6 1.2 %pad_bitcast_fusion.refs_6_ = s32[1,128]{1,0:T(1,128)} fusion(s32[96]{0:T(128)} %param.15), kind=kLoop, calls=%fused_computation | loop fusion | bytes 896 | tf_op jit(solution)/shard_map/reshape | solution.py:603
  1.8 25.5 %coupled.1 = (f32[3072,128]{1,0:T(8,128)}, f32[384,128]{1,0:T(8,128)}) custom-call(f32[3072,128]{1,0:T(8,128)} %bitcast.15, f32[3072,128]{1,0:T(8,128)} %bitcast.16, f32[32,128]{1,0:T(8,128)} %bitcast.20, f32[384,128]{1,0:T(8,128)} %bitcast.18, f32[384,128]{1,0:T(8,128)} %bitcast.19, f32[16,128]{1,0:T(8,128)} %bitcast.21, s32[1,128]{1,0:T(1,128)} %pad_bitcast_fusion.refs_6_, ...), custom_call_target="tpu_custom_call" | custom-call | tf_op jit(solution)/shard_map/coupled/pallas_call | solution.py:587
  27.3 0.0 copy-start
  27.3 2.7 %copy.13 = f32[1,32,96,128]{3,2,1,0:T(8,128)} copy(f32[1,32,96,128]{3,2,1,0:T(8,128)} %bitcast.14) | data formatting | bytes 3145728
  30.0 0.0 copy-done
  30.0 0.7 %copy.14 = f32[1,16,24,128]{3,2,1,0:T(8,128)} copy(f32[1,16,24,128]{3,2,1,0:T(8,128)S(1)} %bitcast.17) | data formatting | bytes 393216
Async XLA Ops:
  27.3 2.7 %copy-start = (f32[384,128]{1,0:T(8,128)S(1)}, f32[384,128]{1,0:T(8,128)}, u32[]{:S(2)}) copy-start(f32[384,128]{1,0:T(8,128)} %get-tuple-element.5) | copy-start | bytes 589828

commit v2 on v1

--- a/solution.py
+++ b/solution.py
@@ -28,6 +28,11 @@
 def split_terms(v):
     head = v.astype(BF16)
     return jnp.concatenate([head, (v - head.astype(F32)).astype(BF16)], axis=1)
+
+
+def band(tt):
+    apart = (lax.broadcasted_iota(jnp.int32, (2 * FZ, FZ), 0) & (FZ - 1)) - lane_iota((2 * FZ, FZ))
+    tt[...] = jnp.where((apart == 1) | (apart == -1), 1.0, 0.0).astype(BF16)
 
 
 def zsum_by_product(values, tt):
@@ -113,8 +118,8 @@
 def kernel(
     n_grp, n_dom,
     fs, fr, fc, ss, sr, sc, sb, ts, tf,
-    fo, so,
-    p, q, a, b, bt, sp, sq, sa, sbb, sbt,
+    p, q, a, b, bt, sp,
+    sq, sa, sbb, sbt,
     mt, yy, xf0, xf1, xf2, xr, xa, xb, xs0, xs1, xsr, xsa, xsb,
     dx, vv, ww, pad, tpad, fin, sin, sins, fxx, fsx, xoff,
     fcv, scv, sbv, tt,
@@ -157,8 +162,7 @@
             )
 
     sends = []
-    apart = (lax.broadcasted_iota(jnp.int32, (2 * FZ, FZ), 0) & (FZ - 1)) - lane_iota((2 * FZ, FZ))
-    tt[...] = jnp.where((apart == 1) | (apart == -1), 1.0, 0.0).astype(BF16)
+    band(tt)
 
     def send(src, dst, index, peer):
         copy = pltpu.make_async_remote_copy(
@@ -347,7 +351,8 @@
         dx[k, pl.ds(16, 80), :] = to_f32(wl[k])
         dx[k, pl.ds(192, 80), :] = to_f32(wr[k])
     for n, ref in enumerate((sbl, sbv, sbr)):
-        spread = jnp.broadcast_to(ref[...].astype(F32), (FZ, FZ)).T
+        row = jnp.concatenate([ref[...].astype(F32), jnp.zeros((1, FZ - SEG), F32)], axis=1)
+        spread = jnp.broadcast_to(row, (FZ, FZ)).T
         xoff[pl.ds(n * SEG, SEG), :] = spread[:SEG].astype(jnp.int32)
     first = SX * (d + n_dom - 1) - 2
     zone = SX * n_dom
@@ -492,10 +497,6 @@
         patch(i, None)
     second = (0, 0, 1, 1)
     interior(second)
-    out_mid = pltpu.make_async_copy(
-        p.at[pl.ds(8 * FY, 24 * FY)], fo.at[pl.ds(4 * FY, 24 * FY)], load_sem.at[19]
-    )
-    out_mid.start()
 
     for name in ("scbl", "scbr", "shlr", "shrr", "sinr"):
         recv[name].wait_recv()
@@ -528,8 +529,6 @@
             [[((src, (x - 1) * SY), (src, x * SY), (src, (x + 1) * SY), (dst, x * SY)) for x in rows]],
             3, 1, tt[...], lambda n, tile: sa[pl.ds(rows[n] * SY + 8 * tile, 8), :], fixed,
         )
-    out_solid = pltpu.make_async_copy(sp.at[pl.ds(8 * SY, SX * SY)], so, load_sem.at[20])
-    out_solid.start()
 
     recv["mhlr"].wait_recv()
     recv["mhrr"].wait_recv()
@@ -538,17 +537,52 @@
     for i in range(4):
         patch(i, ml)
         patch(36 + i, mr)
-    edges(second)
-    outs = []
-    for n, i in enumerate((4, 32)):
-        copy = pltpu.make_async_copy(
-            p.at[pl.ds(i * FY, 4 * FY)], fo.at[pl.ds((i - 4) * FY, 4 * FY)], load_sem.at[21 + n]
-        )
-        copy.start()
-        outs.append(copy)
     for copy in sends:
         copy.wait_send()
-    for copy in (out_mid, out_solid, *outs):
+
+
+def finish(p, q, a, b, bt, sp, fo, so, rows, tt, sem):
+    copies = [
+        pltpu.make_async_copy(p.at[pl.ds(8 * FY, 24 * FY)], fo.at[pl.ds(4 * FY, 24 * FY)], sem.at[0]),
+        pltpu.make_async_copy(sp.at[pl.ds(8 * SY, SX * SY)], so, sem.at[1]),
+    ]
+    for copy in copies:
+        copy.start()
+    band(tt)
+    for m in range(4):
+        groups, xs = [], []
+        for side, x0 in ((0, 1 + m), (1, 35 - m)):
+            def at(x, side=side):
+                lo = (m, 36 - m)[side]
+                if m and lo <= x < lo + 4:
+                    return rows, ((m - 1) * 8 + side * 4 + x - lo) * FY
+                return (p, q)[m % 2], x * FY
+
+            groups.append(
+                [
+                    (at(x - 1), at(x), at(x + 1), (rows, (m * 8 + side * 4 + x - x0) * FY))
+                    for x in range(x0, x0 + 4)
+                ]
+            )
+            xs.extend(range(x0, x0 + 4))
+
+        def fixed(n, tile):
+            if tile == 0:
+                return bt[pl.ds((m // 2) * 320 + xs[n] * 8, 8), :]
+            return b[pl.ds(xs[n] * FY + 8 * tile, 8), :]
+
+        sweep_rows(
+            groups, 12, 6, tt[...], lambda n, tile: a[pl.ds(xs[n] * FY + 8 * tile, 8), :], fixed
+        )
+    for side, x in ((0, 0), (1, 28)):
+        copies.append(
+            pltpu.make_async_copy(
+                rows.at[pl.ds((24 + 4 * side) * FY, 4 * FY)],
+                fo.at[pl.ds(x * FY, 4 * FY)], sem.at[2 + side],
+            )
+        )
+        copies[-1].start()
+    for copy in copies:
         copy.wait()
 
 
@@ -557,20 +591,19 @@
 
 
 SCRATCH = [
-    *(vm(40 * FY, FZ) for _ in range(4)), vm(2 * 320, FZ),
-    *(vm(32 * SY, FZ) for _ in range(4)), vm(4 * 256, FZ),
+    *(vm(32 * SY, FZ) for _ in range(3)), vm(4 * 256, FZ),
     vm(2 * SEG * FZ, FZ, dtype=BF16), vm(2 * SEG * 8, FZ),
     *(vm(96 * 8, FZ) for _ in range(6)), *(vm(48 * 8, FZ) for _ in range(5)),
     vm(6, 3 * SEG, FZ), vm(30, 40, FZ), vm(30, 40, FZ), vm(3, 64, FZ), vm(5, 64, FZ),
     vm(12, 40, FZ), vm(6, 40, FZ), vm(4, 32, FZ), vm(96, FZ), vm(32, FZ),
     vm(3 * SEG, FZ, dtype=jnp.int32),
-    vm(FX, FZ), vm(SX, FZ), vm(1, FZ, dtype=jnp.int32), vm(2 * FZ, FZ, dtype=BF16),
+    vm(FX, FZ), vm(SX, FZ), vm(1, SEG, dtype=jnp.int32), vm(2 * FZ, FZ, dtype=BF16),
     vm(2, 256, FZ, dtype=BF16), vm(2, 128, FZ, dtype=BF16), vm(6, SEG, FZ, dtype=BF16),
     vm(7 * FY, FZ, dtype=BF16), vm(7 * FY, FZ, dtype=BF16),
     vm(2, 8 * SY, FZ, dtype=BF16), vm(2, 8 * SY, FZ, dtype=BF16),
     vm(4 * FY, FZ, dtype=BF16), vm(4 * FY, FZ, dtype=BF16),
     vm(2, 192, FZ, dtype=BF16), vm(2, 192, FZ, dtype=BF16), vm(FX, FZ), vm(FX, FZ),
-    vm(1, FZ, dtype=jnp.int32), vm(1, FZ, dtype=jnp.int32),
+    vm(1, SEG, dtype=jnp.int32), vm(1, SEG, dtype=jnp.int32),
     *(vm(2, 128, FZ, dtype=BF16) for _ in range(3)), *(vm(SX, FZ) for _ in range(5)),
     vm(6, 80, FZ, dtype=BF16), vm(6, 80, FZ, dtype=BF16),
     vm(7 * FY, FZ, dtype=BF16), vm(7 * FY, FZ, dtype=BF16),
@@ -580,29 +613,43 @@
 ]
 
 
+STATE = (*(vm(40 * FY, FZ) for _ in range(4)), vm(2 * 320, FZ), vm(32 * SY, FZ))
+
+
 def solution(mesh):
     n_grp, n_dom = mesh.shape["grp"], mesh.shape["dom"]
 
     def local(fs, fr, fc, ss, sr, sc, sb, ts, tf):
-        fo, so = pl.pallas_call(
+        state = pl.pallas_call(
             lambda *refs: kernel(n_grp, n_dom, *refs),
-            out_shape=(
-                jax.ShapeDtypeStruct((FX * FY, FZ), F32),
-                jax.ShapeDtypeStruct((SX * SY, FZ), F32),
-            ),
-            in_specs=[pl.BlockSpec(memory_space=pl.ANY)] * 9,
-            out_specs=[pl.BlockSpec(memory_space=pl.ANY)] * 2,
+            out_shape=STATE,
+            in_specs=[pl.BlockSpec(memory_space=pltpu.HBM)] * 9,
+            out_specs=tuple(pl.BlockSpec(memory_space=pltpu.VMEM) for _ in STATE),
             scratch_shapes=SCRATCH,
             compiler_params=pltpu.CompilerParams(
-                collective_id=0, has_side_effects=True, vmem_limit_bytes=56 * 1024 * 1024
+                collective_id=0, has_side_effects=True, vmem_limit_bytes=58_458_112
             ),
             name="coupled",
         )(
             fs.reshape(FX * FY, FZ), fr.reshape(FX * FY, FZ), fc.reshape(FX, FZ),
             ss.reshape(SX * SY, FZ), sr.reshape(SX * SY, FZ), sc.reshape(SX, FZ),
-            jnp.pad(sb, (0, FZ - SEG)).reshape(1, FZ),
+            sb.reshape(1, SEG),
             ts.reshape(SEG * FZ, FZ), tf.reshape(SEG * FZ, FZ),
         )
+        fo, so = pl.pallas_call(
+            finish,
+            out_shape=(
+                jax.ShapeDtypeStruct((FX * FY, FZ), F32),
+                jax.ShapeDtypeStruct((SX * SY, FZ), F32),
+            ),
+            in_specs=[pl.BlockSpec(memory_space=pltpu.VMEM)] * 6,
+            out_specs=[pl.BlockSpec(memory_space=pltpu.HBM)] * 2,
+            scratch_shapes=[
+                vm(32 * FY, FZ), vm(2 * FZ, FZ, dtype=BF16), pltpu.SemaphoreType.DMA((4,))
+            ],
+            compiler_params=pltpu.CompilerParams(vmem_limit_bytes=16 * 1024 * 1024),
+            name="finish",
+        )(*state)
         return fo.reshape(1, FX, FY, FZ), so.reshape(1, SX, SY, FZ)
 
     cells = P("grp", "dom", None, None)

time: 30.8 us -> 26.4 us (0.86)
  local copies, waits for them, and re-layouts: 4.55 us -> 0 us
    unnamed x4 -> x0, local copies, waits for them, and re-layouts: 3.38 us -> none
    reshape x1 -> x0, local copies, waits for them, and re-layouts: 1.17 us -> none  [local(): jnp.pad(sb, (0, FZ - SEG)).reshape(1, FZ)]
    pallas_call x1 -> x2, Pallas kernels: 25.5 us -> 25.7 us  [the longest x1 24 us: local(): pl.pallas_call(lambda *refs: kernel(n_grp, n_dom, *refs), out_shape=STATE...]
where the time goes in v2:
time: 26.4 us; the launch traced here: 26.3 us
  Pallas kernels  25.7 us (97%)
  between operations  0.64 us (2%)
    pallas_call x1, Pallas kernels, local(): pl.pallas_call(lambda *refs: kernel(n_grp, n_dom, *refs), out_shape=STATE...  24 us
    pallas_call x1, Pallas kernels, local(): pl.pallas_call(finish, out_shape=(jax.ShapeDtypeStruct((FX * FY, FZ), F32...  1.67 us

profile of v2, /device:TPU:0, one launch (start us, length us, event | category | flops | bytes accessed | tf_op | source)
XLA Modules:
  0.0 26.3 jit_solution(1914395167170003058)
XLA Ops:
  0.6 24.0 %coupled.1 = (f32[3840,128]{1,0:T(8,128)S(1)}, f32[3840,128]{1,0:T(8,128)S(1)}, f32[3840,128]{1,0:T(8,128)S(1)}, f32[3840,128]{1,0:T(8,128)S(1)}, f32[640,128]{1,0:T(8,128)S(1)}, /*index=5*/f32[768,128]{1,0:T(8,128)S(1)}) custom-call(f32[3072,128]{1,0:T(8,128)} %bitcast.13, f32[3072,128]{1,0:T(8,128)} %bitcast.14, f32[32,128]{1,0:T(8,128)} %bitcast.17, ...), custom_call_target="tpu_custom_call" | custom-call | tf_op jit(solution)/shard_map/coupled/pallas_call | solution.py:623
  24.7 1.7 %finish.1 = (f32[3072,128]{1,0:T(8,128)}, f32[384,128]{1,0:T(8,128)}) custom-call(f32[3840,128]{1,0:T(8,128)S(1)} %get-tuple-element.10.p, f32[3840,128]{1,0:T(8,128)S(1)} %get-tuple-element.11.q, f32[3840,128]{1,0:T(8,128)S(1)} %get-tuple-element.12.a, f32[3840,128]{1,0:T(8,128)S(1)} %get-tuple-element.13.b, f32[640,128]{1,0:T(8,128)S(1)} %get-tuple-element.14.bt, ...), custom_call_target="tpu_custom_call" | custom-call | tf_op jit(solution)/shard_map/finish/pallas_call | solution.py:639

commit v3 on v2

--- a/solution.py
+++ b/solution.py
@@ -118,13 +118,12 @@
 def kernel(
     n_grp, n_dom,
     fs, fr, fc, ss, sr, sc, sb, ts, tf,
-    p, q, a, b, bt, sp,
-    sq, sa, sbb, sbt,
-    mt, yy, xf0, xf1, xf2, xr, xa, xb, xs0, xs1, xsr, xsa, xsb,
+    p, q, a, b, bt, sp, sa, sbb, sbt,
+    mt, xf0, xf1, xf2, xr, xa, xb, xs0, xs1, xsr, xsa, xsb,
     dx, vv, ww, pad, tpad, fin, sin, sins, fxx, fsx, xoff,
     fcv, scv, sbv, tt,
-    ifs, is_, wb, bhl, bhr, shl, shr, mhl, mhr,
-    rfl, rfr, fcl, fcr, sbl, sbr, rso, rsr, rsl, sco, scr, scl, scbr, scbl,
+    ifl, ifr, is_, wb, bhl, bhr, shl, shr, mhl, mhr,
+    rfl, rfr, sbl, sbr, rso, rsr, rsl,
     wr, wl, bhrr, bhlr, shrr, shlr, mhrr, mhlr, sinr,
     load_sem, send_sem, recv_sem,
 ):
@@ -148,112 +147,78 @@
 
     load("ss", ss, sp.at[pl.ds(8 * SY, SX * SY)], 0)
     load("sr", sr, sa.at[pl.ds(8 * SY, SX * SY)], 1)
-    load("fs", fs, p.at[pl.ds(4 * FY, FX * FY)], 2)
-    load("fr", fr, a.at[pl.ds(4 * FY, FX * FY)], 3)
     load("sc", sc, scv, 4)
     load("fc", fc, fcv, 5)
     load("sb", sb, sbv, 6)
-    chunk = GROUP * FZ
+    load("fs", fs, p.at[pl.ds(4 * FY, FX * FY)], 2)
+    load("fr", fr, a.at[pl.ds(4 * FY, FX * FY)], 3)
     for t, src in ((0, ts), (1, tf)):
-        for c in (0, 3, 1, 4, 2, 5):
-            load(
-                ("m", t, c), src.at[pl.ds(c * chunk, chunk)],
-                mt.at[pl.ds((t * SEG * FZ) + c * chunk, chunk)], 7 + t * 6 + c,
-            )
+        load(("m", t), src, mt.at[pl.ds(t * SEG * FZ, SEG * FZ)], 7 + t)
 
     sends = []
+    inner_left, inner_right = d > 0, d < n_dom - 1
     band(tt)
 
-    def send(src, dst, index, peer):
+    def send(src, dst, index, peer, when=None, got=None):
         copy = pltpu.make_async_remote_copy(
             src_ref=src, dst_ref=dst, send_sem=send_sem.at[index], recv_sem=recv_sem.at[index],
             device_id=peer, device_id_type=MESH,
         )
-        copy.start()
-        sends.append(copy)
-        return copy
+        if when is None:
+            copy.start()
+        else:
+            pl.when(when)(copy.start)
+        sends.append((copy, when))
+        return copy.wait_recv if got is None else lambda: pl.when(got)(copy.wait_recv)
+
+    @pl.when(d == 0)
+    def _():
+        for ref in (bhlr, shlr, mhlr):
+            ref[...] = jnp.zeros(ref.shape, BF16)
+
+    @pl.when(d == n_dom - 1)
+    def _():
+        for ref in (bhrr, shrr, mhrr):
+            ref[...] = jnp.zeros(ref.shape, BF16)
 
     loads["ss"].wait()
     loads["sr"].wait()
+    loads["sc"].wait()
     for f, ref in ((0, sp), (1, sa)):
         for i in range(SX // 2):
             lo = (8 + 2 * i) * SY + 16
-            is_[f, pl.ds(16 * i, 16), :] = jnp.concatenate(
+            is_[pl.ds(128 * f + 16 * i, 16), :] = jnp.concatenate(
                 [ref[pl.ds(lo, 8), :], ref[pl.ds(lo + SY, 8), :]], axis=0
             ).astype(BF16)
-        shl[f] = ref[pl.ds(8 * SY, 8 * SY), :].astype(BF16)
-        shr[f] = ref[pl.ds(16 * SY, 8 * SY), :].astype(BF16)
-    loads["fs"].wait()
-    loads["fr"].wait()
-    for f, ref in ((0, p), (1, a)):
-        for i in range(FX // 2):
-            lo = (4 + 2 * i) * FY
-            pair = jnp.concatenate([ref[pl.ds(lo, 8), :], ref[pl.ds(lo + FY, 8), :]], axis=0)
-            ifs[f, pl.ds(16 * i, 16), :] = pair.astype(BF16)
-            own = xf0 if f == 0 else xr
-            own[pl.ds((FX + 2 * i) * 8, 16), :] = pair
-    loads["sc"].wait()
-    loads["fc"].wait()
-    loads["sb"].wait()
-    pl.semaphore_wait(barrier, 8)
-
-    recv = {}
-    recv["rso"] = send(is_, rso, 6, (gm, d))
-    recv["rsr"] = send(is_, rsr, 7, (gm, dm))
-    recv["rsl"] = send(is_, rsl, 8, (gm, dp))
-    recv["rfr"] = send(ifs.at[:, pl.ds(0, 192)], rfr, 0, (g, dm))
-    recv["rfl"] = send(ifs.at[:, pl.ds(64, 192)], rfl, 1, (g, dp))
-    recv["fcr"] = send(fcv, fcr, 2, (g, dm))
-    recv["fcl"] = send(fcv, fcl, 3, (g, dp))
-    recv["sbr"] = send(sbv, sbr, 4, (g, dm))
-    recv["sbl"] = send(sbv, sbl, 5, (g, dp))
-    recv["sco"] = send(scv, sco, 9, (gm, d))
-    recv["scr"] = send(scv, scr, 10, (gm, dm))
-    recv["scl"] = send(scv, scl, 11, (gm, dp))
-    recv["scbr"] = send(scv, scbr, 12, (g, dm))
-    recv["scbl"] = send(scv, scbl, 13, (g, dp))
-
-    prow = lax.broadcasted_iota(jnp.int32, (8, 2 * FZ), 0)
-    pcol = lane_iota((8, 2 * FZ))
-    wanted = jnp.where(pcol < FZ, lax.rem(pcol, 3), lax.rem(pcol - FZ, 3) + 3)
-    probe = jnp.where(wanted == prow, 1.0, 0.0).astype(BF16)
-    phase = lax.rem(lane_iota((24, FZ)), 3)
-    for t in range(2):
-        for c in range(3):
-            loads[("m", t, c)].wait()
-            loads[("m", t, 3 + c)].wait()
-            for v in range(8 * c, 8 * c + 8):
-                at = (t * SEG + 2 * v) * FZ
-                four = jnp.concatenate(
-                    [mt[pl.ds(at, 2 * FZ), :], mt[pl.ds(at + 48 * FZ, 2 * FZ), :]], axis=1
-                )
-                found = jnp.dot(probe, four, preferred_element_type=F32)
-                yy[pl.ds(t * 384 + v * 8, 8), :] = found[:, :FZ]
-                yy[pl.ds(t * 384 + 192 + v * 8, 8), :] = found[:, FZ:]
-        for h in range(2):
-            for e in range(2):
-                y3 = [
-                    yy[pl.ds(t * 384 + h * 192 + 3 * e + c, 24, stride=8), :] for c in range(3)
-                ]
-                for k, shift in enumerate((0, 2, 1)):
-                    picked = jnp.where(phase == 1, y3[(1 + shift) % 3], y3[shift])
-                    picked = jnp.where(phase == 2, y3[(2 + shift) % 3], picked)
-                    dx[3 * t + k, pl.ds(SEG + 48 * h + e, 24, stride=2), :] = picked
-        for k in range(3):
-            wb[3 * t + k] = dx[3 * t + k, pl.ds(SEG, SEG), :].astype(BF16)
-    recv["wr"] = send(wb.at[:, pl.ds(0, 80)], wr, 14, (g, dm))
-    recv["wl"] = send(wb.at[:, pl.ds(16, 80)], wl, 15, (g, dp))
-
-    for i in range(4):
-        bhl[pl.ds(i * FY, FY), :] = p[pl.ds((4 + i) * FY, FY), :].astype(BF16)
-        bhr[pl.ds(i * FY, FY), :] = p[pl.ds((32 + i) * FY, FY), :].astype(BF16)
-    for i in range(3):
-        bhl[pl.ds((4 + i) * FY, FY), :] = a[pl.ds((4 + i) * FY, FY), :].astype(BF16)
-        bhr[pl.ds((4 + i) * FY, FY), :] = a[pl.ds((33 + i) * FY, FY), :].astype(BF16)
-    recv["bhrr"] = send(bhl, bhrr, 16, (g, dm))
-    recv["bhlr"] = send(bhr, bhlr, 17, (g, dp))
-    recv["shrr"] = send(shl, shrr, 18, (g, dm))
-    recv["shlr"] = send(shr, shlr, 19, (g, dp))
+        shl[pl.ds(192 * f, 192), :] = ref[pl.ds(8 * SY, 8 * SY), :].astype(BF16)
+        shr[pl.ds(192 * f, 192), :] = ref[pl.ds(16 * SY, 8 * SY), :].astype(BF16)
+    is_[pl.ds(256, SX), :] = scv[...].astype(BF16)
+    shl[pl.ds(384, SX), :] = scv[...].astype(BF16)
+    shr[pl.ds(384, SX), :] = scv[...].astype(BF16)
+
+    def fluid_ready():
+        loads["fs"].wait()
+        loads["fr"].wait()
+        loads["fc"].wait()
+        loads["sb"].wait()
+        for f, ref in ((0, p), (1, a)):
+            for i in range(FX // 2):
+                lo = (4 + 2 * i) * FY
+                pair = jnp.concatenate([ref[pl.ds(lo, 8), :], ref[pl.ds(lo + FY, 8), :]], axis=0)
+                if i < 12:
+                    ifl[pl.ds(192 * f + 16 * i, 16), :] = pair.astype(BF16)
+                if i >= 4:
+                    ifr[pl.ds(192 * f + 16 * (i - 4), 16), :] = pair.astype(BF16)
+                own = xf0 if f == 0 else xr
+                own[pl.ds((FX + 2 * i) * 8, 16), :] = pair
+        for ref in (ifl, ifr):
+            ref[pl.ds(384, FX), :] = fcv[...].astype(BF16)
+        for i in range(4):
+            bhl[pl.ds(i * FY, FY), :] = p[pl.ds((4 + i) * FY, FY), :].astype(BF16)
+            bhr[pl.ds(i * FY, FY), :] = p[pl.ds((32 + i) * FY, FY), :].astype(BF16)
+        for i in range(3):
+            bhl[pl.ds((4 + i) * FY, FY), :] = a[pl.ds((4 + i) * FY, FY), :].astype(BF16)
+            bhr[pl.ds((4 + i) * FY, FY), :] = a[pl.ds((33 + i) * FY, FY), :].astype(BF16)
 
     def coef(start_ref, rate_ref, a_ref, b_ref, lo, size):
         r = rate_ref[pl.ds(lo, size), :]
@@ -264,12 +229,6 @@
     def film_coef(r0, s0, film):
         inv0 = 1.0 / (1.0 + 6.0 * r0 + film)
         return r0 * inv0, s0 * inv0, film * inv0
-
-    own_rows = pl.ds(4 * FY, FX, stride=FY)
-    a0, b0, _ = film_coef(a[own_rows, :], p[own_rows, :], fcv[...])
-    rows_loop(4, 36, 4, lambda x: coef(p, a, a, b, at_row(x, FY), FY))
-    a[own_rows, :] = a0
-    b[own_rows, :] = b0
 
     def fluid_sweep(src, dst, variant, spans):
         groups, bases, rows = [], [], []
@@ -291,8 +250,9 @@
             groups, 12, 6, tt[...], lambda n, tile: a[pl.ds(bases[n] + 8 * tile, 8), :], fixed
         )
 
-    def interior(variants):
-        for m, block in enumerate((10, 7, 13, 8)):
+    def interior(variants, sweeps=range(4)):
+        for m in sweeps:
+            block = (10, 7, 13, 8)[m]
             src, dst = (p, q) if m % 2 == 0 else (q, p)
 
             def step(i, carry):
@@ -306,18 +266,84 @@
             src, dst = (p, q) if m % 2 == 0 else (q, p)
             fluid_sweep(src, dst, variants[m], ((1 + m, 4), (35 - m, 4)))
 
-    interior((None,) * 4)
-
-    recv["rfl"].wait_recv()
-    recv["rfr"].wait_recv()
-    recv["fcl"].wait_recv()
-    recv["fcr"].wait_recv()
+    def local_work():
+        own_rows = pl.ds(4 * FY, FX, stride=FY)
+        a0, b0, _ = film_coef(a[own_rows, :], p[own_rows, :], fcv[...])
+        rows_loop(4, 36, 4, lambda x: coef(p, a, a, b, at_row(x, FY), FY))
+        a[own_rows, :] = a0
+        b[own_rows, :] = b0
+        interior((None,) * 4, range(1))
+        folded_row = lax.broadcasted_iota(jnp.int32, (16, FZ), 0)
+        folded_col = lane_iota((16, FZ))
+        masks = [
+            jnp.where(((folded_col + shift) & 15) == folded_row, 1.0, 0.0).astype(BF16)
+            for shift in (0, 15, 1)
+        ]
+        owner = lax.broadcasted_iota(jnp.int32, (GROUP, GROUP * 16), 1) // 16
+        gather = jnp.where(
+            owner == lax.broadcasted_iota(jnp.int32, (GROUP, GROUP * 16), 0), 1.0, 0.0
+        ).astype(BF16)
+        for t in range(2):
+            loads[("m", t)].wait()
+            for c in range(SEG // GROUP):
+                folded = []
+                for n in range(GROUP):
+                    at = (t * SEG + c * GROUP + n) * FZ
+                    parts = [mt[pl.ds(at + 16 * r, 16), :] for r in range(8)]
+                    while len(parts) > 1:
+                        parts = [u + v for u, v in zip(parts[::2], parts[1::2])]
+                    folded.append(parts[0])
+                for k in range(3):
+                    picked = jnp.dot(
+                        gather, jnp.concatenate([f * masks[k] for f in folded], axis=0),
+                        preferred_element_type=F32,
+                    )
+                    dx[3 * t + k, pl.ds(SEG + c * GROUP, GROUP), :] = picked
+                    wb[3 * t + k, pl.ds(c * GROUP, GROUP), :] = picked.astype(BF16)
+
+    early = (g == 0) | (d == 0)
+
+    @pl.when(early)
+    def _():
+        fluid_ready()
+        local_work()
+
+    pl.semaphore_wait(barrier, 8)
+    recv = {}
+    recv["rso"] = send(is_, rso, 2, (gm, d))
+    recv["rsr"] = send(is_, rsr, 3, (gm, dm))
+    recv["rsl"] = send(is_, rsl, 4, (gm, dp))
+
+    @pl.when(jnp.logical_not(early))
+    def _():
+        fluid_ready()
+
+    recv["rfr"] = send(ifl, rfr, 0, (g, dm))
+    recv["rfl"] = send(ifr, rfl, 1, (g, dp))
+    recv["sbr"] = send(sbv, sbr, 5, (g, dm))
+    recv["sbl"] = send(sbv, sbl, 6, (g, dp))
+
+    @pl.when(jnp.logical_not(early))
+    def _():
+        local_work()
+
+    recv["wr"] = send(wb.at[:, pl.ds(0, 80)], wr, 7, (g, dm))
+    recv["wl"] = send(wb.at[:, pl.ds(16, 80)], wl, 8, (g, dp))
+    recv["bhrr"] = send(bhl, bhrr, 9, (g, dm), inner_left, inner_right)
+    recv["bhlr"] = send(bhr, bhlr, 10, (g, dp), inner_right, inner_left)
+    recv["shrr"] = send(shl, shrr, 11, (g, dm), inner_left, inner_right)
+    recv["shlr"] = send(shr, shlr, 12, (g, dp), inner_right, inner_left)
+
+    interior((None,) * 4, range(1, 4))
+
+    recv["rfl"]()
+    recv["rfr"]()
     for f, ref in ((0, xf0), (1, xr)):
-        ref[pl.ds(64, 192), :] = to_f32(rfl[f])
-        ref[pl.ds(512, 192), :] = to_f32(rfr[f])
-    fxx[pl.ds(0, FX), :] = fcl[...]
+        ref[pl.ds(64, 192), :] = to_f32(rfl[pl.ds(192 * f, 192), :])
+        ref[pl.ds(512, 192), :] = to_f32(rfr[pl.ds(192 * f, 192), :])
+    fxx[pl.ds(0, FX), :] = to_f32(rfl[pl.ds(384, FX), :])
     fxx[pl.ds(FX, FX), :] = fcv[...]
-    fxx[pl.ds(2 * FX, FX), :] = fcr[...]
+    fxx[pl.ds(2 * FX, FX), :] = to_f32(rfr[pl.ds(384, FX), :])
     rows_loop(1, 11, 2, lambda x: coef(xf0, xr, xa, xb, at_row(x, 64), 64))
     xc = []
     xb0 = []
@@ -331,22 +357,21 @@
         xc.append(2 + par)
         xb0.append(par)
 
-    for name in ("rso", "rsr", "rsl", "sco", "scr", "scl"):
-        recv[name].wait_recv()
+    for name in ("rso", "rsr", "rsl"):
+        recv[name]()
     for f, ref in ((0, xs0), (1, xsr)):
-        ref[pl.ds(0, 128), :] = to_f32(rsl[f])
-        ref[pl.ds(128, 128), :] = to_f32(rso[f])
-        ref[pl.ds(256, 128), :] = to_f32(rsr[f])
+        for n, got in enumerate((rsl, rso, rsr)):
+            ref[pl.ds(128 * n, 128), :] = to_f32(got[pl.ds(128 * f, 128), :])
     rows_loop(0, 6, 2, lambda x: coef(xs0, xsr, xsa, xsb, at_row(x, 64), 64))
     srows = pl.ds(32 + 7, 40, stride=8)
-    film = jnp.concatenate([scl[...], sco[...], scr[...]], axis=0)[4:44]
+    film = jnp.concatenate([to_f32(got[pl.ds(256, SX), :]) for got in (rsl, rso, rsr)], axis=0)[4:44]
     a0, b0, c0 = film_coef(xsr[srows, :], xs0[srows, :], film)
     xsa[srows, :] = a0
     sin[0] = b0
     sin[1] = c0
 
     for name in ("sbl", "sbr", "wl", "wr"):
-        recv[name].wait_recv()
+        recv[name]()
     for k in range(6):
         dx[k, pl.ds(16, 80), :] = to_f32(wl[k])
         dx[k, pl.ds(192, 80), :] = to_f32(wr[k])
@@ -452,17 +477,17 @@
             lo, hi = solid_span[k][n]
             src, dst = (xs0, xs1) if n == 0 else (xs1, xs0)
             face_sweep(src, dst, xsa, xsb, SX, lo, hi)
-    recv["sinr"] = send(sins, sinr, 22, (gp, d))
-
-    recv["bhlr"].wait_recv()
-    recv["bhrr"].wait_recv()
-    for ref, first_row, mask, film_at in ((bhlr, 0, ml, 28), (bhrr, 36, mr, 64)):
+    recv["sinr"] = send(sins, sinr, 13, (gp, d))
+
+    recv["bhlr"]()
+    recv["bhrr"]()
+    for ref, first_row, film_at in ((bhlr, 0, 28), (bhrr, 36, 64)):
         for i in range(4):
-            p[pl.ds((first_row + i) * FY, FY), :] = to_f32(ref[pl.ds(i * FY, FY), :]) * mask
+            p[pl.ds((first_row + i) * FY, FY), :] = to_f32(ref[pl.ds(i * FY, FY), :])
         skip = 1 if first_row == 0 else 0
         for i in range(3):
             row = first_row + skip + i
-            a[pl.ds(row * FY, FY), :] = to_f32(ref[pl.ds((4 + i) * FY, FY), :]) * mask
+            a[pl.ds(row * FY, FY), :] = to_f32(ref[pl.ds((4 + i) * FY, FY), :])
         for i in range(3):
             row = first_row + skip + i
             film = fxx[pl.ds(film_at + skip + i, 1), :]
@@ -474,8 +499,8 @@
     edges((None,) * 4)
     mhl[...] = p[pl.ds(4 * FY, 4 * FY), :].astype(BF16)
     mhr[...] = p[pl.ds(32 * FY, 4 * FY), :].astype(BF16)
-    recv["mhrr"] = send(mhl, mhrr, 20, (g, dm))
-    recv["mhlr"] = send(mhr, mhlr, 21, (g, dp))
+    recv["mhrr"] = send(mhl, mhrr, 14, (g, dm), inner_left, inner_right)
+    recv["mhlr"] = send(mhr, mhlr, 15, (g, dp), inner_right, inner_left)
 
     wide = lax.broadcasted_iota(jnp.int32, (20, FZ), 0)
     inside = jnp.where(wide < 2, ml, jnp.where(wide >= 18, mr, 1.0))
@@ -498,14 +523,14 @@
     second = (0, 0, 1, 1)
     interior(second)
 
-    for name in ("scbl", "scbr", "shlr", "shrr", "sinr"):
-        recv[name].wait_recv()
+    recv["shlr"]()
+    recv["shrr"]()
     for f, ref in ((0, sp), (1, sa)):
-        ref[pl.ds(0, 8 * SY), :] = to_f32(shlr[f]) * ml
-        ref[pl.ds(24 * SY, 8 * SY), :] = to_f32(shrr[f]) * mr
-    fsx[pl.ds(0, 8), :] = scbl[pl.ds(8, 8), :] * ml
+        ref[pl.ds(0, 8 * SY), :] = to_f32(shlr[pl.ds(192 * f, 192), :])
+        ref[pl.ds(24 * SY, 8 * SY), :] = to_f32(shrr[pl.ds(192 * f, 192), :])
+    fsx[pl.ds(0, 8), :] = to_f32(shlr[pl.ds(384, SX), :])[8:]
     fsx[pl.ds(8, SX), :] = scv[...]
-    fsx[pl.ds(24, 8), :] = scbr[pl.ds(0, 8), :] * mr
+    fsx[pl.ds(24, 8), :] = to_f32(shrr[pl.ds(384, SX), :])[:8]
     last_rows = pl.ds(SY - 1, 32, stride=SY)
     a0, b0, c0 = film_coef(sa[last_rows, :], sp[last_rows, :], fsx[...])
     rows_loop(0, 8, 2, lambda x: coef(sp, sa, sa, sbb, at_row(x, 96), 96))
@@ -514,41 +539,46 @@
     for k in range(4):
         for i in range(32):
             sbt[pl.ds(k * 256 + i * 8, 8), :] = sbb[pl.ds(i * SY + 16, 8), :]
+    recv["sinr"]()
+    for k in range(4):
         sbt[pl.ds(k * 256 + 7, 32, stride=8), :] = b0 + c0 * sinr[k]
 
-    for m in range(8):
-        src, dst = (sp, sq) if m % 2 == 0 else (sq, sp)
-        rows = range(1 + m, 31 - m)
-
-        def fixed(n, tile):
-            if tile == 2:
-                return sbt[pl.ds((m // 2) * 256 + rows[n] * 8, 8), :]
-            return sbb[pl.ds(rows[n] * SY + 8 * tile, 8), :]
-
-        sweep_rows(
-            [[((src, (x - 1) * SY), (src, x * SY), (src, (x + 1) * SY), (dst, x * SY)) for x in rows]],
-            3, 1, tt[...], lambda n, tile: sa[pl.ds(rows[n] * SY + 8 * tile, 8), :], fixed,
-        )
-
-    recv["mhlr"].wait_recv()
-    recv["mhrr"].wait_recv()
-    p[pl.ds(0, 4 * FY), :] = to_f32(mhlr[...]) * ml
-    p[pl.ds(36 * FY, 4 * FY), :] = to_f32(mhrr[...]) * mr
+    recv["mhlr"]()
+    recv["mhrr"]()
+    p[pl.ds(0, 4 * FY), :] = to_f32(mhlr[...])
+    p[pl.ds(36 * FY, 4 * FY), :] = to_f32(mhrr[...])
     for i in range(4):
         patch(i, ml)
         patch(36 + i, mr)
-    for copy in sends:
-        copy.wait_send()
-
-
-def finish(p, q, a, b, bt, sp, fo, so, rows, tt, sem):
+    for copy, when in sends:
+        if when is None:
+            copy.wait_send()
+        else:
+            pl.when(when)(copy.wait_send)
+
+
+def finish(p, q, a, b, bt, sp, sa, sbb, sbt, fo, so, rows, s1, s2, tt, sem):
     copies = [
-        pltpu.make_async_copy(p.at[pl.ds(8 * FY, 24 * FY)], fo.at[pl.ds(4 * FY, 24 * FY)], sem.at[0]),
-        pltpu.make_async_copy(sp.at[pl.ds(8 * SY, SX * SY)], so, sem.at[1]),
+        pltpu.make_async_copy(p.at[pl.ds(8 * FY, 24 * FY)], fo.at[pl.ds(4 * FY, 24 * FY)], sem.at[0])
     ]
-    for copy in copies:
-        copy.start()
+    copies[0].start()
     band(tt)
+
+    def solid_sweep(m):
+        span = range(1 + m, 31 - m)
+        src = sp if m == 0 else (s2, s1)[m % 2]
+        dst = (s1, s2)[m % 2]
+
+        def fixed(n, tile):
+            if tile == 2:
+                return sbt[pl.ds((m // 2) * 256 + span[n] * 8, 8), :]
+            return sbb[pl.ds(span[n] * SY + 8 * tile, 8), :]
+
+        sweep_rows(
+            [[((src, (x - 1) * SY), (src, x * SY), (src, (x + 1) * SY), (dst, x * SY)) for x in span]],
+            3, 1, tt[...], lambda n, tile: sa[pl.ds(span[n] * SY + 8 * tile, 8), :], fixed,
+        )
+
     for m in range(4):
         groups, xs = [], []
         for side, x0 in ((0, 1 + m), (1, 35 - m)):
@@ -574,6 +604,10 @@
         sweep_rows(
             groups, 12, 6, tt[...], lambda n, tile: a[pl.ds(xs[n] * FY + 8 * tile, 8), :], fixed
         )
+        solid_sweep(2 * m)
+        solid_sweep(2 * m + 1)
+    copies.append(pltpu.make_async_copy(s2.at[pl.ds(8 * SY, SX * SY)], so, sem.at[1]))
+    copies[-1].start()
     for side, x in ((0, 0), (1, 28)):
         copies.append(
             pltpu.make_async_copy(
@@ -591,29 +625,31 @@
 
 
 SCRATCH = [
-    *(vm(32 * SY, FZ) for _ in range(3)), vm(4 * 256, FZ),
-    vm(2 * SEG * FZ, FZ, dtype=BF16), vm(2 * SEG * 8, FZ),
+    vm(2 * SEG * FZ, FZ, dtype=BF16),
     *(vm(96 * 8, FZ) for _ in range(6)), *(vm(48 * 8, FZ) for _ in range(5)),
     vm(6, 3 * SEG, FZ), vm(30, 40, FZ), vm(30, 40, FZ), vm(3, 64, FZ), vm(5, 64, FZ),
     vm(12, 40, FZ), vm(6, 40, FZ), vm(4, 32, FZ), vm(96, FZ), vm(32, FZ),
     vm(3 * SEG, FZ, dtype=jnp.int32),
     vm(FX, FZ), vm(SX, FZ), vm(1, SEG, dtype=jnp.int32), vm(2 * FZ, FZ, dtype=BF16),
-    vm(2, 256, FZ, dtype=BF16), vm(2, 128, FZ, dtype=BF16), vm(6, SEG, FZ, dtype=BF16),
-    vm(7 * FY, FZ, dtype=BF16), vm(7 * FY, FZ, dtype=BF16),
-    vm(2, 8 * SY, FZ, dtype=BF16), vm(2, 8 * SY, FZ, dtype=BF16),
+    vm(416, FZ, dtype=BF16), vm(416, FZ, dtype=BF16), vm(272, FZ, dtype=BF16),
+    vm(6, SEG, FZ, dtype=BF16), vm(7 * FY, FZ, dtype=BF16), vm(7 * FY, FZ, dtype=BF16),
+    vm(400, FZ, dtype=BF16), vm(400, FZ, dtype=BF16),
     vm(4 * FY, FZ, dtype=BF16), vm(4 * FY, FZ, dtype=BF16),
-    vm(2, 192, FZ, dtype=BF16), vm(2, 192, FZ, dtype=BF16), vm(FX, FZ), vm(FX, FZ),
+    vm(416, FZ, dtype=BF16), vm(416, FZ, dtype=BF16),
     vm(1, SEG, dtype=jnp.int32), vm(1, SEG, dtype=jnp.int32),
-    *(vm(2, 128, FZ, dtype=BF16) for _ in range(3)), *(vm(SX, FZ) for _ in range(5)),
+    *(vm(272, FZ, dtype=BF16) for _ in range(3)),
     vm(6, 80, FZ, dtype=BF16), vm(6, 80, FZ, dtype=BF16),
     vm(7 * FY, FZ, dtype=BF16), vm(7 * FY, FZ, dtype=BF16),
-    vm(2, 8 * SY, FZ, dtype=BF16), vm(2, 8 * SY, FZ, dtype=BF16),
+    vm(400, FZ, dtype=BF16), vm(400, FZ, dtype=BF16),
     vm(4 * FY, FZ, dtype=BF16), vm(4 * FY, FZ, dtype=BF16), vm(4, 32, FZ),
-    pltpu.SemaphoreType.DMA((24,)), pltpu.SemaphoreType.DMA((23,)), pltpu.SemaphoreType.DMA((23,)),
+    pltpu.SemaphoreType.DMA((9,)), pltpu.SemaphoreType.DMA((16,)), pltpu.SemaphoreType.DMA((16,)),
 ]
 
 
-STATE = (*(vm(40 * FY, FZ) for _ in range(4)), vm(2 * 320, FZ), vm(32 * SY, FZ))
+STATE = (
+    *(vm(40 * FY, FZ) for _ in range(4)), vm(2 * 320, FZ),
+    *(vm(32 * SY, FZ) for _ in range(3)), vm(4 * 256, FZ),
+)
 
 
 def solution(mesh):
@@ -627,7 +663,7 @@
             out_specs=tuple(pl.BlockSpec(memory_space=pltpu.VMEM) for _ in STATE),
             scratch_shapes=SCRATCH,
             compiler_params=pltpu.CompilerParams(
-                collective_id=0, has_side_effects=True, vmem_limit_bytes=58_458_112
+                collective_id=0, has_side_effects=True, vmem_limit_bytes=57_147_392
             ),
             name="coupled",
         )(
@@ -642,10 +678,11 @@
                 jax.ShapeDtypeStruct((FX * FY, FZ), F32),
                 jax.ShapeDtypeStruct((SX * SY, FZ), F32),
             ),
-            in_specs=[pl.BlockSpec(memory_space=pltpu.VMEM)] * 6,
+            in_specs=[pl.BlockSpec(memory_space=pltpu.VMEM)] * 9,
             out_specs=[pl.BlockSpec(memory_space=pltpu.HBM)] * 2,
             scratch_shapes=[
-                vm(32 * FY, FZ), vm(2 * FZ, FZ, dtype=BF16), pltpu.SemaphoreType.DMA((4,))
+                vm(32 * FY, FZ), vm(32 * SY, FZ), vm(32 * SY, FZ), vm(2 * FZ, FZ, dtype=BF16),
+                pltpu.SemaphoreType.DMA((4,)),
             ],
             compiler_params=pltpu.CompilerParams(vmem_limit_bytes=16 * 1024 * 1024),
             name="finish",

time: 26.4 us -> 24.1 us (0.913)
  Pallas kernels: 25.7 us -> 23.4 us
    pallas_call x1, Pallas kernels: 24 us -> 20.6 us  [local(): pl.pallas_call(lambda *refs: kernel(n_grp, n_dom, *refs), out_shape=STATE...]
    pallas_call x1, Pallas kernels: 1.67 us -> 2.79 us  [local(): pl.pallas_call(finish, out_shape=(jax.ShapeDtypeStruct((FX * FY, FZ), F32...]
where the time goes in v3:
time: 24.1 us; the launch traced here: 24 us
  Pallas kernels  23.4 us (97%)
  between operations  0.64 us (3%)
    pallas_call x1, Pallas kernels, local(): pl.pallas_call(lambda *refs: kernel(n_grp, n_dom, *refs), out_shape=STATE...  20.6 us
    pallas_call x1, Pallas kernels, local(): pl.pallas_call(finish, out_shape=(jax.ShapeDtypeStruct((FX * FY, FZ), F32...  2.79 us

profile of v3, /device:TPU:0, one launch (start us, length us, event | category | flops | bytes accessed | tf_op | source)
XLA Modules:
  0.0 24.0 jit_solution(9652652401330220274)
XLA Ops:
  0.6 20.6 %coupled.1 = (f32[3840,128]{1,0:T(8,128)S(1)}, f32[3840,128]{1,0:T(8,128)S(1)}, f32[3840,128]{1,0:T(8,128)S(1)}, f32[3840,128]{1,0:T(8,128)S(1)}, f32[640,128]{1...) custom-call(f32[3072,128]{1,0:T(8,128)} %bitcast.13, ...), custom_call_target="tpu_custom_call" | custom-call | tf_op jit(solution)/shard_map/coupled/pallas_call | solution.py:659
  21.3 2.8 %finish.1 = (f32[3072,128]{1,0:T(8,128)}, f32[384,128]{1,0:T(8,128)}) custom-call(f32[3840,128]{1,0:T(8,128)S(1)} %get-tuple-element.13.p, f32[3840,128]{1,0:T(8,128)S(1)} %get-tuple-element.14.q, f32[3840,128]{1,0:T(8,128)S(1)} %get-tuple-element.15.a, f32[3840,128]{1,0:T(8,128)S(1)} %get-tuple-element.16.b, f32[640,128]{1,0:T(8,128)S(1)} %get-tuple-element.17.bt, ...), custom_call_target="tpu_custom_call" | custom-call | tf_op jit(solution)/shard_map/finish/pallas_call | solution.py:675

commit v4 on v3

--- a/solution.py
+++ b/solution.py
@@ -65,16 +65,7 @@
     return x * pitch if isinstance(x, int) else pl.multiple_of(x * pitch, 8)
 
 
-def ysum_tile(ref, at, tile, tiles, cur):
-    zero = jnp.zeros((1, FZ), F32)
-    if 0 < tile < tiles - 1 and tile % 2 == 0:
-        return ref[pl.ds(at - 1, 8), :] + ref[pl.ds(at + 1, 8), :]
-    low = zero if tile == 0 else ref[pl.ds(at - 1, 1), :]
-    high = zero if tile == tiles - 1 else ref[pl.ds(at + 8, 1), :]
-    return jnp.concatenate([low, cur[:-1]], axis=0) + jnp.concatenate([cur[1:], high], axis=0)
-
-
-def sweep_rows(groups, tiles, rolled, tt, coef_a, fixed):
+def sweep_rows(groups, tiles, rolled, tt, coef_a, fixed, loaded=(1, 2, 4, 5, 6, 7, 9, 10)):
     products = []
     for group in groups:
         halves = [group[: len(group) // 2], group[len(group) // 2 :]]
@@ -87,16 +78,37 @@
                 [ref[pl.ds(at + 8 * rolled, height), :] for _, (ref, at), _, _ in part], tt
             )
             products.extend(total[n * height : (n + 1) * height] for n in range(len(part)))
+    held = {}
+
+    def cell(number, row, tile):
+        key = number, row, tile
+        if key not in held:
+            group = groups[number]
+            if row < 0:
+                ref, at = group[0][0]
+            elif row == len(group):
+                ref, at = group[-1][2]
+            else:
+                ref, at = group[row][1]
+            held[key] = ref[pl.ds(at + 8 * tile, 8), :]
+        return held[key]
+
+    zero = jnp.zeros((1, FZ), F32)
     for tile in range(tiles):
         n = 0
-        for group in groups:
-            cur = None
-            for left, row, right, target in group:
-                here = row[1] + 8 * tile
-                before = cur if cur is not None else left[0][pl.ds(left[1] + 8 * tile, 8), :]
-                cur = after if cur is not None else row[0][pl.ds(here, 8), :]
-                after = right[0][pl.ds(right[1] + 8 * tile, 8), :]
-                summed = (before + after) + ysum_tile(row[0], here, tile, tiles, cur)
+        for number, group in enumerate(groups):
+            for row, (_, (ref, at), _, target) in enumerate(group):
+                here = at + 8 * tile
+                cur = cell(number, row, tile)
+                beside = cell(number, row - 1, tile) + cell(number, row + 1, tile)
+                if tile in loaded and tile < tiles - 1:
+                    across = ref[pl.ds(here - 1, 8), :] + ref[pl.ds(here + 1, 8), :]
+                else:
+                    low = zero if tile == 0 else cell(number, row, tile - 1)[7:]
+                    high = zero if tile == tiles - 1 else cell(number, row, tile + 1)[:1]
+                    across = jnp.concatenate([low, cur[:-1]], axis=0)
+                    across = across + jnp.concatenate([cur[1:], high], axis=0)
+                summed = beside + across
                 if tile < rolled:
                     summed = summed + zsum(cur)
                 else:
@@ -159,16 +171,20 @@
     inner_left, inner_right = d > 0, d < n_dom - 1
     band(tt)
 
-    def send(src, dst, index, peer, when=None, got=None):
+    def prepare(src, dst, index, peer, when=None):
         copy = pltpu.make_async_remote_copy(
             src_ref=src, dst_ref=dst, send_sem=send_sem.at[index], recv_sem=recv_sem.at[index],
             device_id=peer, device_id_type=MESH,
         )
+        sends.append((copy, when))
+        return copy
+
+    def send(src, dst, index, peer, when=None, got=None):
+        copy = prepare(src, dst, index, peer, when)
         if when is None:
             copy.start()
         else:
             pl.when(when)(copy.start)
-        sends.append((copy, when))
         return copy.wait_recv if got is None else lambda: pl.when(got)(copy.wait_recv)
 
     @pl.when(d == 0)
@@ -219,6 +235,8 @@
         for i in range(3):
             bhl[pl.ds((4 + i) * FY, FY), :] = a[pl.ds((4 + i) * FY, FY), :].astype(BF16)
             bhr[pl.ds((4 + i) * FY, FY), :] = a[pl.ds((33 + i) * FY, FY), :].astype(BF16)
+        bhl[pl.ds(7 * FY, 16), :] = fcv[pl.ds(0, 16), :].astype(BF16)
+        bhr[pl.ds(7 * FY, 16), :] = fcv[pl.ds(16, 16), :].astype(BF16)
 
     def coef(start_ref, rate_ref, a_ref, b_ref, lo, size):
         r = rate_ref[pl.ds(lo, size), :]
@@ -336,6 +354,38 @@
 
     interior((None,) * 4, range(1, 4))
 
+    at_end = (d == 0) | (d == n_dom - 1)
+    mh_left = prepare(mhl, mhrr, 14, (g, dm), inner_left)
+    mh_right = prepare(mhr, mhlr, 15, (g, dp), inner_right)
+    recv["mhrr"] = lambda: pl.when(inner_right)(mh_left.wait_recv)
+    recv["mhlr"] = lambda: pl.when(inner_left)(mh_right.wait_recv)
+
+    def first_edges():
+        recv["bhlr"]()
+        recv["bhrr"]()
+        for ref, first_row, film_at in ((bhlr, 1, 13), (bhrr, 36, 0)):
+            films = to_f32(ref[pl.ds(7 * FY, 16), :])
+            for i in range(4):
+                row = (0, 36)[first_row == 36] + i
+                p[pl.ds(row * FY, FY), :] = to_f32(ref[pl.ds(i * FY, FY), :])
+            for i in range(3):
+                row = first_row + i
+                a[pl.ds(row * FY, FY), :] = to_f32(ref[pl.ds((4 + i) * FY, FY), :])
+            for i in range(3):
+                row = first_row + i
+                r0, s0 = a[pl.ds(row * FY, 1), :], p[pl.ds(row * FY, 1), :]
+                a0, b0, _ = film_coef(r0, s0, films[film_at + i : film_at + i + 1])
+                coef(p, a, a, b, row * FY, FY)
+                a[pl.ds(row * FY, 1), :] = a0
+                b[pl.ds(row * FY, 1), :] = b0
+        edges((None,) * 4)
+        mhl[...] = p[pl.ds(4 * FY, 4 * FY), :].astype(BF16)
+        mhr[...] = p[pl.ds(32 * FY, 4 * FY), :].astype(BF16)
+        pl.when(inner_left)(mh_left.start)
+        pl.when(inner_right)(mh_right.start)
+
+    pl.when(at_end)(first_edges)
+
     recv["rfl"]()
     recv["rfr"]()
     for f, ref in ((0, xf0), (1, xr)):
@@ -356,19 +406,6 @@
         fin[2 + par] = c0
         xc.append(2 + par)
         xb0.append(par)
-
-    for name in ("rso", "rsr", "rsl"):
-        recv[name]()
-    for f, ref in ((0, xs0), (1, xsr)):
-        for n, got in enumerate((rsl, rso, rsr)):
-            ref[pl.ds(128 * n, 128), :] = to_f32(got[pl.ds(128 * f, 128), :])
-    rows_loop(0, 6, 2, lambda x: coef(xs0, xsr, xsa, xsb, at_row(x, 64), 64))
-    srows = pl.ds(32 + 7, 40, stride=8)
-    film = jnp.concatenate([to_f32(got[pl.ds(256, SX), :]) for got in (rsl, rso, rsr)], axis=0)[4:44]
-    a0, b0, c0 = film_coef(xsr[srows, :], xs0[srows, :], film)
-    xsa[srows, :] = a0
-    sin[0] = b0
-    sin[1] = c0
 
     for name in ("sbl", "sbr", "wl", "wr"):
         recv[name]()
@@ -400,6 +437,19 @@
                     else:
                         vv[at] = total * fin[xc[par]]
 
+    for name in ("rso", "rsr", "rsl"):
+        recv[name]()
+    for f, ref in ((0, xs0), (1, xsr)):
+        for n, got in enumerate((rsl, rso, rsr)):
+            ref[pl.ds(128 * n, 128), :] = to_f32(got[pl.ds(128 * f, 128), :])
+    rows_loop(0, 6, 2, lambda x: coef(xs0, xsr, xsa, xsb, at_row(x, 64), 64))
+    srows = pl.ds(32 + 7, 40, stride=8)
+    film = jnp.concatenate([to_f32(got[pl.ds(256, SX), :]) for got in (rsl, rso, rsr)], axis=0)[4:44]
+    a0, b0, c0 = film_coef(xsr[srows, :], xs0[srows, :], film)
+    xsa[srows, :] = a0
+    sin[0] = b0
+    sin[1] = c0
+
     def shifts(v):
         return (v, pltpu.roll(v, 1, 1), pltpu.roll(v, FZ - 1, 1))
 
@@ -465,6 +515,7 @@
         fluid_ref = (xf0, xf0, xf2, xf0)[k]
         project_fluid(xs0, k)
         project_solid(fluid_ref, k)
+        recv["sinr", k] = send(sins.at[k], sinr.at[k], (13, 16, 17, 18)[k], (gp, d))
         if k == 3:
             break
         for par in range(2):
@@ -477,30 +528,8 @@
             lo, hi = solid_span[k][n]
             src, dst = (xs0, xs1) if n == 0 else (xs1, xs0)
             face_sweep(src, dst, xsa, xsb, SX, lo, hi)
-    recv["sinr"] = send(sins, sinr, 13, (gp, d))
-
-    recv["bhlr"]()
-    recv["bhrr"]()
-    for ref, first_row, film_at in ((bhlr, 0, 28), (bhrr, 36, 64)):
-        for i in range(4):
-            p[pl.ds((first_row + i) * FY, FY), :] = to_f32(ref[pl.ds(i * FY, FY), :])
-        skip = 1 if first_row == 0 else 0
-        for i in range(3):
-            row = first_row + skip + i
-            a[pl.ds(row * FY, FY), :] = to_f32(ref[pl.ds((4 + i) * FY, FY), :])
-        for i in range(3):
-            row = first_row + skip + i
-            film = fxx[pl.ds(film_at + skip + i, 1), :]
-            r0, s0 = a[pl.ds(row * FY, 1), :], p[pl.ds(row * FY, 1), :]
-            a0, b0, _ = film_coef(r0, s0, film)
-            coef(p, a, a, b, row * FY, FY)
-            a[pl.ds(row * FY, 1), :] = a0
-            b[pl.ds(row * FY, 1), :] = b0
-    edges((None,) * 4)
-    mhl[...] = p[pl.ds(4 * FY, 4 * FY), :].astype(BF16)
-    mhr[...] = p[pl.ds(32 * FY, 4 * FY), :].astype(BF16)
-    recv["mhrr"] = send(mhl, mhrr, 14, (g, dm), inner_left, inner_right)
-    recv["mhlr"] = send(mhr, mhlr, 15, (g, dp), inner_right, inner_left)
+
+    pl.when(jnp.logical_not(at_end))(first_edges)
 
     wide = lax.broadcasted_iota(jnp.int32, (20, FZ), 0)
     inside = jnp.where(wide < 2, ml, jnp.where(wide >= 18, mr, 1.0))
@@ -539,7 +568,8 @@
     for k in range(4):
         for i in range(32):
             sbt[pl.ds(k * 256 + i * 8, 8), :] = sbb[pl.ds(i * SY + 16, 8), :]
-    recv["sinr"]()
+    for k in range(4):
+        recv["sinr", k]()
     for k in range(4):
         sbt[pl.ds(k * 256 + 7, 32, stride=8), :] = b0 + c0 * sinr[k]
 
@@ -632,17 +662,17 @@
     vm(3 * SEG, FZ, dtype=jnp.int32),
     vm(FX, FZ), vm(SX, FZ), vm(1, SEG, dtype=jnp.int32), vm(2 * FZ, FZ, dtype=BF16),
     vm(416, FZ, dtype=BF16), vm(416, FZ, dtype=BF16), vm(272, FZ, dtype=BF16),
-    vm(6, SEG, FZ, dtype=BF16), vm(7 * FY, FZ, dtype=BF16), vm(7 * FY, FZ, dtype=BF16),
+    vm(6, SEG, FZ, dtype=BF16), vm(7 * FY + 16, FZ, dtype=BF16), vm(7 * FY + 16, FZ, dtype=BF16),
     vm(400, FZ, dtype=BF16), vm(400, FZ, dtype=BF16),
     vm(4 * FY, FZ, dtype=BF16), vm(4 * FY, FZ, dtype=BF16),
     vm(416, FZ, dtype=BF16), vm(416, FZ, dtype=BF16),
     vm(1, SEG, dtype=jnp.int32), vm(1, SEG, dtype=jnp.int32),
     *(vm(272, FZ, dtype=BF16) for _ in range(3)),
     vm(6, 80, FZ, dtype=BF16), vm(6, 80, FZ, dtype=BF16),
-    vm(7 * FY, FZ, dtype=BF16), vm(7 * FY, FZ, dtype=BF16),
+    vm(7 * FY + 16, FZ, dtype=BF16), vm(7 * FY + 16, FZ, dtype=BF16),
     vm(400, FZ, dtype=BF16), vm(400, FZ, dtype=BF16),
     vm(4 * FY, FZ, dtype=BF16), vm(4 * FY, FZ, dtype=BF16), vm(4, 32, FZ),
-    pltpu.SemaphoreType.DMA((9,)), pltpu.SemaphoreType.DMA((16,)), pltpu.SemaphoreType.DMA((16,)),
+    pltpu.SemaphoreType.DMA((9,)), pltpu.SemaphoreType.DMA((19,)), pltpu.SemaphoreType.DMA((19,)),
 ]
 
 

time: 24.1 us -> 24 us (level)
    pallas_call x1, Pallas kernels: 20.6 us -> 20.4 us  [local(): pl.pallas_call(lambda *refs: kernel(n_grp, n_dom, *refs), out_shape=STATE...]
where the time goes in v4:
time: 24 us; the launch traced here: 23.9 us
  Pallas kernels  23.3 us (97%)
  between operations  0.64 us (3%)
    pallas_call x1, Pallas kernels, local(): pl.pallas_call(lambda *refs: kernel(n_grp, n_dom, *refs), out_shape=STATE...  20.4 us
    pallas_call x1, Pallas kernels, local(): pl.pallas_call(finish, out_shape=(jax.ShapeDtypeStruct((FX * FY, FZ), F32...  2.93 us

profile of v4, /device:TPU:0, one launch (start us, length us, event | category | flops | bytes accessed | tf_op | source)
XLA Modules:
  0.0 23.9 jit_solution(12706133055896325536)
XLA Ops:
  0.6 20.4 %coupled.1 = (f32[3840,128]{1,0:T(8,128)S(1)}, f32[3840,128]{1,0:T(8,128)S(1)}, f32[3840,128]{1,0:T(8,128)S(1)}, f32[3840,128]{1,0:T(8,128)S(1)}, f32[640,128]{1...) custom-call(f32[3072,128]{1,0:T(8,128)} %bitcast.13, ...), custom_call_target="tpu_custom_call" | custom-call | tf_op jit(solution)/shard_map/coupled/pallas_call | solution.py:689
  21.0 2.9 %finish.1 = (f32[3072,128]{1,0:T(8,128)}, f32[384,128]{1,0:T(8,128)}) custom-call(f32[3840,128]{1,0:T(8,128)S(1)} %get-tuple-element.13.p, f32[3840,128]{1,0:T(8,128)S(1)} %get-tuple-element.14.q, f32[3840,128]{1,0:T(8,128)S(1)} %get-tuple-element.15.a, f32[3840,128]{1,0:T(8,128)S(1)} %get-tuple-element.16.b, f32[640,128]{1,0:T(8,128)S(1)} %get-tuple-element.17.bt, ...), custom_call_target="tpu_custom_call" | custom-call | tf_op jit(solution)/shard_map/finish/pallas_call | solution.py:705

commit v5 on v4

--- a/solution.py
+++ b/solution.py
@@ -677,7 +677,7 @@
 
 
 STATE = (
-    *(vm(40 * FY, FZ) for _ in range(4)), vm(2 * 320, FZ),
+    *(vm(40 * FY, FZ) for _ in range(4)), vm(2 * 320 + 64, FZ),
     *(vm(32 * SY, FZ) for _ in range(3)), vm(4 * 256, FZ),
 )
 
@@ -693,7 +693,7 @@
             out_specs=tuple(pl.BlockSpec(memory_space=pltpu.VMEM) for _ in STATE),
             scratch_shapes=SCRATCH,
             compiler_params=pltpu.CompilerParams(
-                collective_id=0, has_side_effects=True, vmem_limit_bytes=57_147_392
+                collective_id=0, has_side_effects=True, vmem_limit_bytes=57_114_624
             ),
             name="coupled",
         )(

time: 24 us -> 24 us (level)
  no operation moved by 1% of the time
where the time goes in v5:
time: 24 us; the launch traced here: 23.9 us
  Pallas kernels  23.3 us (97%)
  between operations  0.64 us (3%)
    pallas_call x1, Pallas kernels, local(): pl.pallas_call(lambda *refs: kernel(n_grp, n_dom, *refs), out_shape=STATE...  20.4 us
    pallas_call x1, Pallas kernels, local(): pl.pallas_call(finish, out_shape=(jax.ShapeDtypeStruct((FX * FY, FZ), F32...  2.93 us

profile of v5, /device:TPU:0, one launch (start us, length us, event | category | flops | bytes accessed | tf_op | source)
XLA Modules:
  0.0 23.9 jit_solution(10228398122967002010)
XLA Ops:
  0.6 20.4 %coupled.1 = (f32[3840,128]{1,0:T(8,128)S(1)}, f32[3840,128]{1,0:T(8,128)S(1)}, f32[3840,128]{1,0:T(8,128)S(1)}, f32[3840,128]{1,0:T(8,128)S(1)}, f32[704,128]{1...) custom-call(f32[3072,128]{1,0:T(8,128)} %bitcast.13, ...), custom_call_target="tpu_custom_call" | custom-call | tf_op jit(solution)/shard_map/coupled/pallas_call | solution.py:689
  21.0 2.9 %finish.1 = (f32[3072,128]{1,0:T(8,128)}, f32[384,128]{1,0:T(8,128)}) custom-call(f32[3840,128]{1,0:T(8,128)S(1)} %get-tuple-element.13.p, f32[3840,128]{1,0:T(8,128)S(1)} %get-tuple-element.14.q, f32[3840,128]{1,0:T(8,128)S(1)} %get-tuple-element.15.a, f32[3840,128]{1,0:T(8,128)S(1)} %get-tuple-element.16.b, f32[704,128]{1,0:T(8,128)S(1)} %get-tuple-element.17.bt, ...), custom_call_target="tpu_custom_call" | custom-call | tf_op jit(solution)/shard_map/finish/pallas_call | solution.py:705
